TPU v7x, 32 devices: a whole 2x2x4 slice. The times are simulated.
32 devices in a mesh: mesh: 4 (over z), rve: 8 (over y, x, core).
Axes of the slice: x: 2, y: 2, z: 4, core: 2. Of those that a mesh axis runs over, the one named last changes fastest.
Arguments:
- displacement: float32 [3, 128], P(None, ('mesh', 'rve')), may hold values from -6 to 6
- shape_grads: float32 [3, 8, 512], P(None, None, ('mesh', 'rve')), may hold values from -2 to 2
- point_weights: float32 [512], P(('mesh', 'rve')), may hold values from 0.5 to 2
- conn: int32 [8, 64], P(None, ('mesh', 'rve')), may hold values from 0 to 47
- halo_nodes: int32 [2, 32], P(None, 'mesh'), may hold values from 0 to 31
- warm_strain: float32 [512, 6, 4096], P(('mesh', 'rve')), may hold values from -4 to 4
- moduli: float32 [512, 2, 4096], P(('mesh', 'rve')), may hold values from 0.2 to 2
- owner: int32 [512], P(('mesh', 'rve')), may hold values from 0 to 7, as said below
- sweeps: int32 [512], P(('mesh', 'rve')), may hold values from 1 to 2, as said below
Outputs:
- nodal_force: float32 [3, 128], P(None, ('mesh', 'rve'))
- gp_stress: float32 [6, 512], P(None, ('mesh', 'rve'))
- micro_strain: float32 [512, 6, 4096], P(('mesh', 'rve'))
Inputs may be any that keep to these rules, and one draw needn't show every extreme that they name: The owner lies in the Gauss point's own mesh row. The 16 Gauss points of one device go 2 each to 8 different owners, and every owner receives exactly 16 Gauss points. `sweeps`: counts may be skewed by owner: all Gauss points of some owners take 2.
All inputs are finite; a program needn't handle non-finite values.
Results may differ from a plain program's by a relative error of at most 0.0003.
Values sent between devices are 32-bit elements; how exact they have to be, the bound alone decides.
No kernel may reach another device: no remote copies, remote signals or barrier semaphores. Data moves between devices by JAX's collectives and lax.ppermute only.
A program may use at most 128 MiB of HBM per device.

v0:
```python
import functools
import math

import jax
import jax.numpy as jnp
import numpy as np
from jax import lax
from jax.experimental import pallas as pl
from jax.experimental.pallas import tpu as pltpu
from jax.sharding import PartitionSpec as P

REF_MODULUS = 1.1
COUPLING = 2.2 / (1.1 * 3.3)
PAIRS = ((0, 0), (1, 1), (2, 2), (1, 2), (0, 2), (0, 1))
F32 = jnp.float32
BF16 = jnp.bfloat16
LANES = 128


def signed_waves(side):
    wave = np.arange(side)
    return np.where(wave < side // 2, wave, wave - side)


def normal_at(kx, ky, kz, side):
    signed = signed_waves(side)
    xi = np.stack([signed[kx % side], signed[ky % side], signed[kz % side]]).astype(np.float64)
    length = np.sqrt((xi * xi).sum(0))
    return np.where(length > 0, xi / np.where(length > 0, length, 1.0), 0.0)


def plane_sets(side):
    packs = []
    for parity in (0, 1):
        reps, selfs, seen = [], [], set()
        for ky in range(parity, side, 2):
            for kz in range(side):
                if (ky, kz) in seen:
                    continue
                mirror = (-ky % side, -kz % side)
                seen.update({(ky, kz), mirror})
                (selfs if mirror == (ky, kz) else reps).append((ky, kz))
        half = len(selfs) // 2
        first = reps + selfs[:half]
        second = reps + selfs[half:]
        packs.append((first, second, len(reps)))
    return packs


def split_table(table):
    high = np.asarray(table, np.float32).astype(jnp.bfloat16)
    low = (np.asarray(table, np.float64) - high.astype(np.float64)).astype(jnp.bfloat16)
    return high, low


def build_tables(side):
    plane = side * side
    half = plane // 2
    ylo, zz = np.divmod(np.arange(half), side)
    scale = 1.0 / (2.2 * side**3)
    forward = np.zeros((2, 2, plane, plane))
    inverse = np.zeros((2, 2, plane, plane))
    normals = np.zeros((2, side // 2, 2, 6, half))
    packs = plane_sets(side)
    for parity in (0, 1):
        kyi, kz = np.divmod(np.arange(half), side)
        ky = 2 * kyi + parity
        angle = 2 * np.pi / side * ((np.outer(ylo, ky) + np.outer(zz, kz)) % side)
        c, s = np.cos(angle), np.sin(angle)
        forward[parity, 1] = np.block([[c, -s], [s, c]])
        inverse[parity, 1] = np.block([[c.T, s.T], [-s.T, c.T]]) * scale
        for kx in range(1, side // 2):
            plus = normal_at(np.full(half, kx), ky, kz, side)
            minus = normal_at(np.full(half, -kx), -ky, -kz, side)
            normals[parity, kx, :, 0:3] = plus
            normals[parity, kx, :, 3:6] = minus
        first, second, pairs = packs[parity]
        columns = np.array(first + second)
        angle = 2 * np.pi / side * (
            (np.outer(ylo, columns[:, 0]) + np.outer(zz, columns[:, 1])) % side
        )
        imag = np.zeros(half, bool)
        imag[half // 2 : half // 2 + pairs] = True
        single = np.zeros(half, bool)
        single[pairs : half // 2] = True
        single[half // 2 + pairs :] = True
        fwd = np.where(imag[None], -np.sin(angle), np.cos(angle))
        inv = (fwd * np.where(single, 1.0, 2.0)[None]).T * scale
        forward[parity, 0, :half, :half] = fwd
        forward[parity, 0, half:, half:] = fwd
        inverse[parity, 0, :half, :half] = inv
        inverse[parity, 0, half:, half:] = inv
        for part, kx in ((0, 0), (1, side // 2)):
            full = np.full(half, kx)
            normals[parity, 0, part, 0:3] = normal_at(full, columns[:, 0], columns[:, 1], side)
            normals[parity, 0, part, 3:6] = normal_at(-full, -columns[:, 0], -columns[:, 1], side)
    fh, fl = split_table(forward)
    ih, il = split_table(inverse)
    return fh, fl, ih, il, normals.astype(np.float32)


def real_transform(values):
    count = len(values)
    if count == 2:
        return [(values[0] + values[1], None), (values[0] - values[1], None)]
    even = real_transform(values[0::2])
    odd = real_transform(values[1::2])
    half = count // 2
    result = [None] * (half + 1)
    result[0] = (even[0][0] + odd[0][0], None)
    result[half] = (even[0][0] - odd[0][0], None)
    for k in range(1, half // 2):
        (er, ei), (orr, oi) = even[k], odd[k]
        angle = 2 * math.pi * k / count
        c, s = math.cos(angle), math.sin(angle)
        if abs(c - s) < 1e-9:
            tr, ti = (orr + oi) * c, (oi - orr) * c
        else:
            tr, ti = orr * c + oi * s, oi * c - orr * s
        result[k] = (er + tr, ei + ti)
        result[half - k] = (er - tr, ti - ei)
    result[half // 2] = (even[half // 2][0], -odd[half // 2][0])
    return result


def real_inverse(spectrum):
    half = len(spectrum) - 1
    count = 2 * half
    if count == 2:
        return [spectrum[0][0] + spectrum[1][0], spectrum[0][0] - spectrum[1][0]]
    even = [None] * (half // 2 + 1)
    odd = [None] * (half // 2 + 1)
    even[0] = (spectrum[0][0] + spectrum[half][0], None)
    odd[0] = (spectrum[0][0] - spectrum[half][0], None)
    for k in range(1, half // 2):
        (ar, ai), (br, bi) = spectrum[k], spectrum[half - k]
        even[k] = (ar + br, ai - bi)
        dr, di = ar - br, ai + bi
        angle = 2 * math.pi * k / count
        c, s = math.cos(angle), math.sin(angle)
        if abs(c - s) < 1e-9:
            odd[k] = ((dr - di) * c, (dr + di) * c)
        else:
            odd[k] = (dr * c - di * s, dr * s + di * c)
    mid_re, mid_im = spectrum[half // 2]
    even[half // 2] = (mid_re * 2.0, None)
    odd[half // 2] = (mid_im * -2.0, None)
    first, second = real_inverse(even), real_inverse(odd)
    result = []
    for a, b in zip(first, second):
        result += [a, b]
    return result


def green(entries, normal):
    n0, n1, n2 = normal
    t0 = entries[0] * n0 + entries[5] * n1 + entries[4] * n2
    t1 = entries[5] * n0 + entries[1] * n1 + entries[3] * n2
    t2 = entries[4] * n0 + entries[3] * n1 + entries[2] * n2
    load = (n0 * t0 + n1 * t1 + n2 * t2) * (COUPLING * 1.1)
    u0, u1, u2 = t0 - n0 * load, t1 - n1 * load, t2 - n2 * load
    return (
        n0 * u0, n1 * u1, n2 * u2,
        n1 * u2 + n2 * u1, n0 * u2 + n2 * u0, n0 * u1 + n1 * u0,
    )


def split_rows(value):
    high = value.astype(BF16)
    return high, (value - high.astype(F32)).astype(BF16)


def product(high, low, table_high, table_low):
    dot = functools.partial(jnp.dot, preferred_element_type=F32)
    return dot(high, table_high) + (dot(low, table_high) + dot(high, table_low))


def column_to_row(column, diagonal):
    return jnp.sum(jnp.where(diagonal, column, 0.0), axis=0, keepdims=True)


def row_to_column(row, diagonal):
    return jnp.sum(jnp.where(diagonal, row, 0.0), axis=1, keepdims=True)


def main_kernel(
    dims,
    part_ref, ids_ref, conn_ref, grads_ref, table_ref, warm_ref, lame_ref, shear_ref,
    fh_ref, fl_ref, ih_ref, il_ref, normals_ref,
    send_ref, stress_ref, force_ref,
    field, tau, lamb, shear, high, low, spec,
):
    points, comps, side, devices, node_dev, halo, row_span, nodes_part, owners, dense = dims
    voxels = side**3
    plane = side * side
    tiles = voxels // LANES
    rows = comps * points
    slabs = side // 2
    part = part_ref[0]

    lane = lax.broadcasted_iota(jnp.int32, (points, LANES), 1)
    sub = lax.broadcasted_iota(jnp.int32, (points, LANES), 0)
    diagonal = lane == sub
    owner_row = ids_ref[0:1, :]
    sweeps_row = ids_ref[1:2, :]
    weight_row = ids_ref[2:3, :]
    valid = lane < points
    if dense:
        owner_col = row_to_column(owner_row, diagonal)
        earlier = jnp.where((owner_col == owner_row) & (lane < sub), 1.0, 0.0)
        rank_col = jnp.sum(earlier, axis=1, keepdims=True)
        slot_row = column_to_row(rank_col * owners + owner_col, diagonal)
        choose = jnp.where((slot_row == sub.astype(F32)) & valid, 1.0, 0.0)
    else:
        choose = jnp.where(diagonal, 1.0, 0.0)
    pick_col = jnp.sum(choose * lane.astype(F32), axis=1, keepdims=True).astype(jnp.int32)
    count_col = jnp.sum(choose * sweeps_row, axis=1, keepdims=True)

    exch = table_ref[...]
    dev_sub = lax.broadcasted_iota(jnp.int32, exch.shape, 0)
    below = jnp.sum(jnp.where(dev_sub == (part - 1) * row_span, exch, 0.0), axis=0, keepdims=True)
    above = jnp.sum(jnp.where(dev_sub == (part + 1) * row_span, exch, 0.0), axis=0, keepdims=True)
    parts = devices // row_span
    width = nodes_part + 2 * halo
    wide = table_ref.shape[1]
    elane = lax.broadcasted_iota(jnp.int32, (1, wide), 1)
    lane_f = elane.astype(F32)
    part_f = part.astype(F32)
    span = float(nodes_part)
    low_id = jnp.where(part > 0, below + (part_f - 1.0) * span, -1.0)
    high_id = jnp.where(part < parts - 1, above + (part_f + 1.0) * span, -1.0)
    node_row = jnp.where(
        elane < nodes_part,
        part_f * span + lane_f,
        jnp.where(elane < nodes_part + halo, low_id, high_id),
    )
    links = conn_ref[...]
    node_col = jnp.sum(jnp.where(links == elane, node_row, 0.0), axis=1, keepdims=True)
    device_col = jnp.floor(node_col * (1.0 / node_dev))
    inner_col = node_col - device_col * node_dev
    nlinks = links.shape[0]
    hit_lane = lax.broadcasted_iota(jnp.int32, (nlinks, devices), 1).astype(F32)
    hit = jnp.where(hit_lane == device_col, 1.0, 0.0)
    flat_lane = lax.broadcasted_iota(jnp.int32, (nlinks, LANES), 1)
    group = flat_lane // node_dev
    inside = jnp.where(
        ((flat_lane - group * node_dev).astype(F32) == inner_col) & (group < 3), 1.0, 0.0
    )
    fetched = jnp.dot(hit, exch[:, :LANES], preferred_element_type=F32,
                      precision=lax.Precision.HIGHEST) * inside
    moved = [
        jnp.sum(jnp.where(group == i, fetched, 0.0), axis=1, keepdims=True) for i in range(3)
    ]
    elements = points // 8
    glane = lax.broadcasted_iota(jnp.int32, (8, LANES), 1)
    spread = []
    for i in range(3):
        acc = jnp.zeros((8, LANES), F32)
        for e in range(elements):
            acc = jnp.where(glane // 8 == e, moved[i][8 * e : 8 * e + 8], acc)
        spread.append(acc)
    grads = [grads_ref[j] for j in range(3)]
    grad = [
        [jnp.sum(spread[i] * grads[j], axis=0, keepdims=True) for j in range(3)] for i in range(3)
    ]
    macro_rows = [grad[0][0], grad[1][1], grad[2][2]] + [
        (grad[a][b] + grad[b][a]) * 0.5 for a, b in PAIRS[3:]
    ]
    macro_cols = [jnp.sum(choose * row, axis=1, keepdims=True) for row in macro_rows]

    octets = points // 8
    picks = [
        jnp.broadcast_to(pick_col[8 * o : 8 * o + 8], (8, LANES)) for o in range(octets)
    ]

    def gather(ref_value):
        if not dense:
            return ref_value
        outs = []
        for o in range(octets):
            best = None
            for source in range(octets):
                local = jnp.clip(picks[o] - 8 * source, 0, 7)
                got = jnp.take_along_axis(
                    ref_value[8 * source : 8 * source + 8], local, axis=0,
                    mode="promise_in_bounds",
                )
                best = got if best is None else jnp.where(picks[o] >= 8 * source, got, best)
            outs.append(best)
        return jnp.concatenate(outs, axis=0)

    def load_step(t, sums):
        at = pl.ds(pl.multiple_of(t * LANES, LANES), LANES)
        new = []
        for c in range(comps):
            value = gather(warm_ref[c, :, at])
            field[t, c * points : (c + 1) * points] = value
            new.append(sums[c] + value)
        lamb[t] = gather(lame_ref[:, at]) - REF_MODULUS
        shear[t] = gather(shear_ref[:, at]) * 2.0 - 2.0 * REF_MODULUS
        return tuple(new)

    zero = jnp.zeros((points, LANES), F32)
    sums = lax.fori_loop(0, tiles, load_step, (zero,) * comps)
    shift = [
        jnp.broadcast_to(
            macro_cols[c] - jnp.sum(sums[c], axis=1, keepdims=True) * (1.0 / voxels),
            (points, LANES),
        )
        for c in range(comps)
    ]
    macro = jnp.concatenate(
        [jnp.broadcast_to(col, (points, LANES)) for col in macro_cols], axis=0
    )
    group_rows = 16
    groups = rows // group_rows

    def tau_stage(first):
        def step(t, carry):
            eps = []
            for c in range(comps):
                at = slice(c * points, (c + 1) * points)
                value = field[t, at]
                if first:
                    value = value + shift[c]
                    field[t, at] = value
                eps.append(value)
            extra = lamb[t] * (eps[0] + eps[1] + eps[2])
            mu = shear[t]
            for c in range(comps):
                value = mu * eps[c]
                tau[t, c * points : (c + 1) * points] = value + extra if c < 3 else value
            return carry

        lax.fori_loop(0, tiles, step, 0)

    def forward_step(g, carry):
        at = pl.ds(pl.multiple_of(g * group_rows, group_rows), group_rows)
        for parity in (0, 1):
            values = []
            for x in range(side):
                a, b = tau[2 * x, at], tau[2 * x + 1, at]
                values.append(a + b if parity == 0 else a - b)
            out = real_transform(values)
            for s in range(slabs):
                re, im = out[s] if s else (out[0][0], out[slabs][0])
                for k, v in ((0, re), (1, im)):
                    hi, lo = split_rows(v)
                    high[parity, s, at, k * LANES : (k + 1) * LANES] = hi
                    low[parity, s, at, k * LANES : (k + 1) * LANES] = lo
        return carry

    def multiply(th_ref, tl_ref):
        for parity in (0, 1):
            spec[parity, 0] = product(
                high[parity, 0], low[parity, 0], th_ref[parity, 0], tl_ref[parity, 0]
            )
            spec[parity, 1:] = product(
                high[parity, 1:].reshape((slabs - 1) * rows, plane),
                low[parity, 1:].reshape((slabs - 1) * rows, plane),
                th_ref[parity, 1], tl_ref[parity, 1],
            ).reshape(slabs - 1, rows, plane)

    def green_step(index, carry):
        parity = index // slabs
        s = index - parity * slabs
        for k in (0, 1):
            lanes = slice(k * LANES, (k + 1) * LANES)
            table = [
                jnp.broadcast_to(normals_ref[parity, s, k, d : d + 1, :], (8, LANES))
                for d in range(6)
            ]
            results = [[] for _ in range(comps)]
            for o in range(octets):
                entries = [
                    spec[parity, s, c * points + 8 * o : c * points + 8 * o + 8, lanes]
                    for c in range(comps)
                ]
                plus = green(entries, table[0:3])
                minus = green(entries, table[3:6])
                for c in range(comps):
                    value = plus[c] + minus[c]
                    results[c].append(value if c < 3 else value * 0.5)
            for c in range(comps):
                hi, lo = split_rows(jnp.concatenate(results[c], axis=0))
                high[parity, s, c * points : (c + 1) * points, lanes] = hi
                low[parity, s, c * points : (c + 1) * points, lanes] = lo
        return carry

    def inverse_stage(sweep_index):
        for g in range(groups):
            at = slice(g * group_rows, (g + 1) * group_rows)
            base = macro[at]
            mask = jnp.broadcast_to(count_col > float(sweep_index), (points, LANES))
            for yhi in (0, 1):
                parts_k = []
                for s in range(slabs):
                    both = []
                    for k in (0, 1):
                        lanes = slice(k * LANES, (k + 1) * LANES)
                        e, o = spec[0, s, at, lanes], spec[1, s, at, lanes]
                        both.append(e + o if yhi == 0 else e - o)
                    parts_k.append(both)
                spectrum = [(parts_k[0][0], None)] + [tuple(b) for b in parts_k[1:]]
                spectrum.append((parts_k[0][1], None))
                for x, v in enumerate(real_inverse(spectrum)):
                    tile = 2 * x + yhi
                    field[tile, at] = jnp.where(mask, base - v, field[tile, at])

    for sweep_index in (0, 1):
        tau_stage(sweep_index == 0)
        lax.fori_loop(0, groups, forward_step, 0)
        multiply(fh_ref, fl_ref)
        lax.fori_loop(0, 2 * slabs, green_step, 0)
        multiply(ih_ref, il_ref)
        inverse_stage(sweep_index)

    per_owner = points // owners if dense else points

    def stress_step(t, acc):
        eps = [field[t, c * points : (c + 1) * points] for c in range(comps)]
        extra = (lamb[t] + REF_MODULUS) * (eps[0] + eps[1] + eps[2])
        mu = shear[t] + 2.0 * REF_MODULUS
        new = [acc[0] + extra] + [acc[c + 1] + mu * eps[c] for c in range(comps)]
        for c in range(comps):
            if dense:
                for j in range(per_owner):
                    start = (j * comps + c) * tiles + t
                    send_ref[pl.ds(start, owners, stride=per_owner * comps * tiles), :] = (
                        eps[c][j * owners : (j + 1) * owners]
                    )
            else:
                send_ref[c, :, pl.ds(pl.multiple_of(t * LANES, LANES), LANES)] = eps[c]
        return tuple(new)

    acc = lax.fori_loop(0, tiles, stress_step, (zero,) * (comps + 1))
    mean = [jnp.sum(a, axis=1, keepdims=True) * (1.0 / voxels) for a in acc]
    stress_cols = [mean[c + 1] + mean[0] if c < 3 else mean[c + 1] for c in range(comps)]
    stress_rows = [
        jnp.sum(choose * col, axis=0, keepdims=True) for col in stress_cols
    ]
    for c in range(comps):
        stress_ref[c : c + 1, :] = stress_rows[c]

    index_of = ((0, 5, 4), (5, 1, 3), (4, 3, 2))
    weighted = [row * weight_row for row in stress_rows]
    loads = jnp.zeros((nlinks, LANES), F32)
    for i in range(3):
        total = sum(grads[j] * weighted[index_of[i][j]] for j in range(3))
        columns = [
            jnp.sum(jnp.where(glane // 8 == e, total, 0.0), axis=1, keepdims=True)
            for e in range(elements)
        ]
        loads = jnp.where(group == i, jnp.concatenate(columns, axis=0), loads)
    loads = loads * inside
    force_ref[...] = lax.dot_general(
        hit, loads, (((0,), (0,)), ((), ())), preferred_element_type=F32,
        precision=lax.Precision.HIGHEST,
    )


def unpack_kernel(dims, recv_ref, out_ref):
    points, comps, tiles = dims

    def step(t, carry):
        at = pl.ds(pl.multiple_of(t * LANES, LANES), LANES)
        for c in range(comps):
            for h in range(points // 8):
                start = 8 * h * comps * tiles + c * tiles + t
                out_ref[c, 8 * h : 8 * h + 8, at] = recv_ref[
                    pl.ds(start, 8, stride=comps * tiles), :
                ]
        return carry

    lax.fori_loop(0, tiles, step, 0)


def on_device(
    displacement, shape_grads, point_weights, conn, halo_nodes, warm_strain, moduli, owner, sweeps
):
    axes = ("mesh", "rve")
    points, comps, voxels = warm_strain.shape
    side = round(voxels ** (1.0 / 3.0))
    tiles = voxels // LANES
    owners = lax.axis_size("rve")
    devices = lax.axis_size("mesh") * owners
    node_dev = displacement.shape[1]
    nodes_part = node_dev * owners
    halo = halo_nodes.shape[1]
    per_owner = max(2, points // owners)
    dense = per_owner * owners == points and owners == 8
    wide = -(-(nodes_part + 2 * halo) // LANES) * LANES

    row = jnp.zeros((wide,), F32)
    row = row.at[: 3 * node_dev].set(displacement.reshape(-1))
    row = row.at[nodes_part : nodes_part + halo].set(halo_nodes[1].astype(F32))
    row = row.at[nodes_part + halo : nodes_part + 2 * halo].set(halo_nodes[0].astype(F32))
    table = lax.all_to_all(
        jnp.broadcast_to(row[None], (devices, wide)), axes, split_axis=0, concat_axis=0, tiled=True
    )

    ids = jnp.stack([owner.astype(F32), sweeps.astype(F32), point_weights])
    ids = jnp.pad(ids, ((0, 5), (0, LANES - points)))
    elements = conn.shape[1]
    links = jnp.broadcast_to(conn.T.reshape(-1, 1), (8 * elements, wide))
    grads = jnp.pad(shape_grads, ((0, 0), (0, 0), (0, LANES - points)))
    part = lax.axis_index("mesh").astype(jnp.int32).reshape(1)
    warm = warm_strain.transpose(1, 0, 2)
    lame, shear = moduli[:, 0], moduli[:, 1]
    fh, fl, ih, il, normals = build_tables(side)
    dims = (points, comps, side, devices, node_dev, halo, owners, nodes_part, owners, dense)
    rows = comps * points
    plane = side * side
    vmem = pl.BlockSpec(memory_space=pltpu.VMEM)
    if dense:
        send_shape = (points * comps * tiles, LANES)
    else:
        send_shape = (comps, points, voxels)
    send, stress, force = pl.pallas_call(
        functools.partial(main_kernel, dims),
        out_shape=(
            jax.ShapeDtypeStruct(send_shape, F32),
            jax.ShapeDtypeStruct((8, LANES), F32),
            jax.ShapeDtypeStruct((devices, LANES), F32),
        ),
        in_specs=[pl.BlockSpec(memory_space=pltpu.SMEM)] + [vmem] * 12,
        out_specs=(vmem, vmem, vmem),
        scratch_shapes=[
            pltpu.VMEM((tiles, rows, LANES), F32),
            pltpu.VMEM((tiles, rows, LANES), F32),
            pltpu.VMEM((tiles, points, LANES), F32),
            pltpu.VMEM((tiles, points, LANES), F32),
            pltpu.VMEM((2, side // 2, rows, plane), BF16),
            pltpu.VMEM((2, side // 2, rows, plane), BF16),
            pltpu.VMEM((2, side // 2, rows, plane), F32),
        ],
        compiler_params=pltpu.CompilerParams(vmem_limit_bytes=48 << 20),
        name="relax",
    )(part, ids, links, grads, table, warm, lame, shear, fh, fl, ih, il, normals)

    comps_out = stress[:comps, :points]
    pieces = lax.all_to_all(force, axes, split_axis=0, concat_axis=0, tiled=True)
    nodal = jnp.sum(pieces, axis=0)[: 3 * node_dev].reshape(3, node_dev)
    if dense:
        received = lax.all_to_all(send, "rve", split_axis=0, concat_axis=0, tiled=True)
        micro = pl.pallas_call(
            functools.partial(unpack_kernel, (points, comps, tiles)),
            out_shape=jax.ShapeDtypeStruct((comps, points, voxels), F32),
            in_specs=[vmem],
            out_specs=vmem,
            compiler_params=pltpu.CompilerParams(vmem_limit_bytes=16 << 20),
            name="unpack",
        )(received).transpose(1, 0, 2)
    else:
        slots = owners * per_owner
        final = send.transpose(1, 0, 2)
        order = jnp.arange(points, dtype=jnp.int32)
        same = owner[:, None] == owner[None, :]
        rank = jnp.sum((same & (order[None, :] < order[:, None])).astype(jnp.int32), axis=1)
        slot = owner * per_owner + rank
        fields = jnp.zeros((slots, comps, voxels), F32).at[slot].set(final)
        flags = jnp.zeros((slots,), F32).at[slot].set(1.0)
        fields = lax.all_to_all(fields, "rve", split_axis=0, concat_axis=0, tiled=True)
        flags = lax.all_to_all(flags, "rve", split_axis=0, concat_axis=0, tiled=True)
        filled = jnp.nonzero(flags > 0.5, size=points)[0].astype(jnp.int32)
        micro = fields[filled]
    return (nodal, comps_out, micro)


def solution(mesh):
    both = ("mesh", "rve")
    in_specs = (
        P(None, both), P(None, None, both), P(both), P(None, both), P(None, "mesh"),
        P(both, None, None), P(both, None, None), P(both), P(both),
    )
    out_specs = (P(None, both), P(None, both), P(both, None, None))
    return jax.shard_map(
        on_device, mesh=mesh, in_specs=in_specs, out_specs=out_specs, check_vma=False
    )
```

profile of v0, /device:TPU:0, one launch (start us, length us, event | category | flops | bytes accessed | tf_op | source)
XLA Modules:
  0.0 70.6 jit_solution(10003132416090349073)
XLA Ops:
  0.6 0.0 copy-start.1
  0.7 0.9 %reshape.111 = f32[12]{0:T(128)S(1)} reshape(f32[3,4]{1,0:T(4,128)} %param.20) | data formatting | bytes 96 | tf_op jit(solution)/shard_map/reshape.41
  1.6 0.8 %bitcast_dynamic-update-slice_fusion.1 = f32[128]{0:T(128)S(1)} fusion(f32[128]{0:T(128)S(1)} %scatter.10, s32[2,8]{1,0:T(2,128)} %param.24), kind=kLoop, calls=%fused_computation.7 | loop fusion | flops 8 | bytes 544 | tf_op jit(solution)/shard_map/scatter | solution.py:496
  2.4 0.8 %bitcast_dynamic-update-slice_fusion = f32[128]{0:T(128)S(1)} fusion(f32[128]{0:T(128)S(1)} %bitcast_dynamic-update-slice_fusion.1, s32[2,8]{1,0:T(2,128)} %param.24), kind=kLoop, calls=%fused_computation.6 | loop fusion | flops 8 | bytes 544 | tf_op jit(solution)/shard_map/scatter | solution.py:497
  3.1 0.6 broadcast_in_dim.16
  3.7 7.3 %all-to-all-start = ((f32[32,1,128]{2,1,0:T(1,128)}), f32[32,1,128]{2,1,0:T(1,128)S(1)}, u32[]{:S(2)}, u32[]{:S(2)}) async-start(f32[32,1,128]{2,1,0:T(1,128)} %broadcast_in_dim.16), calls=%async_computation | async-start | bytes 32768 | tf_op jit(solution)/shard_map/all_to_all | solution.py:498
  11.1 1.8 %fusion = (f32[16,1,4096]{2,1,0:T(1,128)S(1)}, f32[16,1,4096]{2,1,0:T(1,128)S(1)}) fusion(f32[16,2,4096]{2,1,0:T(2,128)} %param.26), kind=kLoop, calls=%fused_computation.10 | loop fusion | bytes 1048576 | tf_op jit(solution)/shard_map/slice | solution.py:509
  12.9 0.7 convert_bitcast_fusion
  13.5 0.3 copy_bitcast_fusion
  13.9 0.1 broadcast_in_dim.6
  14.0 0.7 %pad.16.grads_ref = f32[3,8,128]{2,1,0:T(8,128)S(1)} pad(f32[3,8,16]{2,1,0:T(8,128)} %param.21, f32[]{:T(128)} %constant.92.clone.1), padding=0_0x0_0x0_112 | pad | bytes 13828 | tf_op jit(solution)/shard_map/jit(_pad)/pad | solution.py:506
  14.7 3.5 %all-to-all-done = f32[32,1,128]{2,1,0:T(1,128)S(1)} async-done(((f32[32,1,128]{2,1,0:T(1,128)}), f32[32,1,128]{2,1,0:T(1,128)S(1)}, u32[]{:S(2)}, u32[]{:S(2)}) %all-to-all-start) | async-done | bytes 16416 | tf_op jit(solution)/shard_map/all_to_all | solution.py:498
  18.2 0.1 broadcast_in_dim.7.conn_ref
  18.3 0.0 copy-start.2
  18.3 1.0 %copy-done.2 = bf16[2,2,256,256]{3,2,1,0:T(8,128)(2,1)S(1)} copy-done((bf16[2,2,256,256]{3,2,1,0:T(8,128)(2,1)S(1)}, bf16[2,2,256,256]{3,2,1,0:T(8,128)(2,1)}, u32[]{:S(2)}) %copy-start.2) | copy-done | bytes 524312
  19.3 1.0 %copy-done.3 = bf16[2,2,256,256]{3,2,1,0:T(8,128)(2,1)S(1)} copy-done((bf16[2,2,256,256]{3,2,1,0:T(8,128)(2,1)S(1)}, bf16[2,2,256,256]{3,2,1,0:T(8,128)(2,1)}, u32[]{:S(2)}) %copy-start.3) | copy-done | bytes 524312
  20.4 1.0 %copy-done.4 = bf16[2,2,256,256]{3,2,1,0:T(8,128)(2,1)S(1)} copy-done((bf16[2,2,256,256]{3,2,1,0:T(8,128)(2,1)S(1)}, bf16[2,2,256,256]{3,2,1,0:T(8,128)(2,1)}, u32[]{:S(2)}) %copy-start.4) | copy-done | bytes 524312
  21.4 12.5 %relax.1 = (f32[3072,128]{1,0:T(8,128)}, f32[8,128]{1,0:T(8,128)}, f32[32,128]{1,0:T(8,128)S(1)}) custom-call(s32[1]{0:T(128)} %bitcast.part_ref, f32[8,128]{1,0:T(8,128)S(1)} %select_maximum_fusion.ids_ref, s32[16,128]{1,0:T(8,128)S(1)} %broadcast_in_dim.7.conn_ref, f32[3,8,128]{2,1,0:T(8,128)S(1)} %pad.16.grads_ref, f32[32,128]{1,0:T(8,128)S(1)} %bitcast.27, ...), custom_call_target="tpu_custom_call" | custom-call | tf_op jit(solution)/shard_map/relax/pallas_call | solution.py:519
  33.9 9.3 %all_to_all.28 = f32[32,1,128]{2,1,0:T(1,128)S(1)} all-to-all(f32[32,1,128]{2,1,0:T(1,128)S(1)} %bitcast.28), channel_id=1, replica_groups=mesh['mesh'=4,'rve'=8] {'mesh','rve'}, dimensions={0} | all-to-all | bytes 32768 | tf_op jit(solution)/shard_map/all_to_all | solution.py:542
  43.2 3.6 %all-to-all-start.2 = ((f32[8,384,128]{2,1,0:T(8,128)}), f32[8,384,128]{2,1,0:T(8,128)S(1)}, u32[]{:S(2)}, u32[]{:S(2)}) async-start(f32[8,384,128]{2,1,0:T(8,128)} %bitcast.13), calls=%async_computation.2 | async-start | bytes 3145728 | tf_op jit(solution)/shard_map/all_to_all | solution.py:545
  46.8 0.1 reduce_sum.9
  46.9 0.7 reshape.112
  47.5 20.2 %all-to-all-done.2 = f32[8,384,128]{2,1,0:T(8,128)S(1)} async-done(((f32[8,384,128]{2,1,0:T(8,128)}), f32[8,384,128]{2,1,0:T(8,128)S(1)}, u32[]{:S(2)}, u32[]{:S(2)}) %all-to-all-start.2) | async-done | bytes 1572896 | tf_op jit(solution)/shard_map/all_to_all | solution.py:545
  67.8 2.9 %unpack.1 = f32[6,16,4096]{2,1,0:T(8,128)} custom-call(f32[3072,128]{1,0:T(8,128)S(1)} %bitcast.25), custom_call_target="tpu_custom_call" | custom-call | tf_op jit(solution)/shard_map/unpack/pallas_call | solution.py:546
  (13 shorter events, 0.0 us)
Async XLA Ops:
  0.6 17.6 %copy-start.5 = (f32[2,8,2,6,128]{4,3,2,1,0:T(8,128)S(1)}, f32[2,8,2,6,128]{4,3,2,1,0:T(8,128)}, u32[]{:S(2)}) copy-start(f32[2,8,2,6,128]{4,3,2,1,0:T(8,128)} %constant.99.clone.normals_ref) | copy-start | bytes 294916
  0.6 17.6 %copy-start.1 = (bf16[2,2,256,256]{3,2,1,0:T(8,128)(2,1)S(1)}, bf16[2,2,256,256]{3,2,1,0:T(8,128)(2,1)}, u32[]{:S(2)}) copy-start(bf16[2,2,256,256]{3,2,1,0:T(8,128)(2,1)} %constant.98.clone.il_ref) | copy-start | bytes 1572868
  0.7 13.2 %copy-start.6 = (f32[16]{0:T(128)S(1)}, f32[16]{0:T(128)}, u32[]{:S(2)}) copy-start(f32[16]{0:T(128)} %param.22) | copy-start | bytes 196
  0.7 13.2 %copy-start.7 = (s32[8,2]{0,1:T(2,128)S(1)}, s32[8,2]{0,1:T(2,128)}, u32[]{:S(2)}) copy-start(s32[8,2]{0,1:T(2,128)} %param.23) | copy-start | bytes 196
  0.7 17.6 %copy-start = (f32[16,6,4096]{2,0,1:T(8,128)S(1)}, f32[16,6,4096]{2,0,1:T(8,128)}, u32[]{:S(2)}) copy-start(f32[16,6,4096]{2,0,1:T(8,128)} %param.25) | copy-start | bytes 4718596
  3.7 14.4 %all-to-all-start = ((f32[32,1,128]{2,1,0:T(1,128)}), f32[32,1,128]{2,1,0:T(1,128)S(1)}, u32[]{:S(2)}, u32[]{:S(2)}) async-start(f32[32,1,128]{2,1,0:T(1,128)} %broadcast_in_dim.16), calls=%async_computation | async-start | bytes 32768 | tf_op jit(solution)/shard_map/all_to_all | solution.py:498
  18.3 1.0 %copy-start.2 = (bf16[2,2,256,256]{3,2,1,0:T(8,128)(2,1)S(1)}, bf16[2,2,256,256]{3,2,1,0:T(8,128)(2,1)}, u32[]{:S(2)}) copy-start(bf16[2,2,256,256]{3,2,1,0:T(8,128)(2,1)} %constant.97.clone.ih_ref) | copy-start | bytes 1572868
  19.3 1.0 %copy-start.3 = (bf16[2,2,256,256]{3,2,1,0:T(8,128)(2,1)S(1)}, bf16[2,2,256,256]{3,2,1,0:T(8,128)(2,1)}, u32[]{:S(2)}) copy-start(bf16[2,2,256,256]{3,2,1,0:T(8,128)(2,1)} %constant.96.clone.fl_ref) | copy-start | bytes 1572868
  20.4 1.0 %copy-start.4 = (bf16[2,2,256,256]{3,2,1,0:T(8,128)(2,1)S(1)}, bf16[2,2,256,256]{3,2,1,0:T(8,128)(2,1)}, u32[]{:S(2)}) copy-start(bf16[2,2,256,256]{3,2,1,0:T(8,128)(2,1)} %constant.95.clone.fh_ref) | copy-start | bytes 1572868
  43.2 24.5 %all-to-all-start.2 = ((f32[8,384,128]{2,1,0:T(8,128)}), f32[8,384,128]{2,1,0:T(8,128)S(1)}, u32[]{:S(2)}, u32[]{:S(2)}) async-start(f32[8,384,128]{2,1,0:T(8,128)} %bitcast.13), calls=%async_computation.2 | async-start | bytes 3145728 | tf_op jit(solution)/shard_map/all_to_all | solution.py:545
where the time goes:
time: 71.1 us; the launch traced here: 70.6 us
  waiting for transfers between devices  23.7 us (33%)
  Pallas kernels  15.4 us (22%)
  starting transfers between devices  10.9 us (15%)
  blocking collectives  9.31 us (13%)
  local copies, waits for them, and re-layouts  8.29 us (12%)
  other arithmetic  2.26 us (3%)
  between operations  0.75 us (1%)
    all_to_all x1, waiting for transfers between devices, on_device(): lax.all_to_all(send, 'rve', split_axis=0, concat_axis=0, tiled=True)  20.2 us
    pallas_call x1, Pallas kernels, on_device(): pl.pallas_call(functools.partial(main_kernel, dims), out_shape=(jax.Shape...  12.5 us
    all_to_all x1, blocking collectives, on_device(): lax.all_to_all(force, axes, split_axis=0, concat_axis=0, tiled=True)  9.31 us
    all_to_all x1, starting transfers between devices, on_device(): lax.all_to_all(jnp.broadcast_to(row[None], (devices, wide)), axes, split_...  7.33 us
    all_to_all x1, starting transfers between devices, on_device(): lax.all_to_all(send, 'rve', split_axis=0, concat_axis=0, tiled=True)  3.58 us
    all_to_all x1, waiting for transfers between devices, on_device(): lax.all_to_all(jnp.broadcast_to(row[None], (devices, wide)), axes, split_...  3.5 us
    unnamed x16, local copies, waits for them, and re-layouts  3.15 us
    pallas_call x1, Pallas kernels, on_device(): pl.pallas_call(functools.partial(unpack_kernel, (points, comps, tiles)),...  2.87 us
  transfers between devices with their start and end apart: 2, of which 2 were waited for; matrix products, arithmetic and copies ran while one was open for 6% of the time, Pallas kernels for 0%

commit v1 on v0

v1 whole, which is shorter than its diff:
```python
import functools
import math

import jax
import jax.numpy as jnp
import numpy as np
from jax import lax
from jax.experimental import pallas as pl
from jax.experimental.pallas import tpu as pltpu
from jax.sharding import PartitionSpec as P


REF_MODULUS = 1.1
COUPLING = 2.2 / (1.1 * 3.3)
PAIRS = ((0, 0), (1, 1), (2, 2), (1, 2), (0, 2), (0, 1))
F32 = jnp.float32
BF16 = jnp.bfloat16
LANES = 128
WINDOW = 32
SPLIT = 24
PREV_LANE = 16
NEXT_LANE = 32


def signed_waves(side):
    wave = np.arange(side)
    return np.where(wave < side // 2, wave, wave - side)


def normal_at(kx, ky, kz, side):
    signed = signed_waves(side)
    xi = np.stack([signed[kx % side], signed[ky % side], signed[kz % side]]).astype(np.float64)
    length = np.sqrt((xi * xi).sum(0))
    return np.where(length > 0, xi / np.where(length > 0, length, 1.0), 0.0)


def plane_sets(side):
    packs = []
    for parity in (0, 1):
        columns, seen = [], set()
        for ky in range(parity, side, 2):
            for kz in range(side):
                if (ky, kz) in seen:
                    continue
                mirror = (-ky % side, -kz % side)
                seen.update({(ky, kz), mirror})
                if mirror == (ky, kz):
                    columns.append((ky, kz, 0, 1))
                else:
                    columns += [(ky, kz, 0, 0), (ky, kz, 1, 0)]
        packs.append(np.array(columns))
    return packs


def window_order(parity, at_edge):
    edge, rest = list(np.flatnonzero(at_edge)), list(np.flatnonzero(~at_edge))
    lead = SPLIT if parity else 0
    limit = WINDOW - SPLIT if parity else SPLIT
    assert len(edge) <= limit
    return np.array(rest[:lead] + edge + rest[lead:])


def split_table(table):
    high = np.asarray(table, np.float32).astype(jnp.bfloat16)
    low = (np.asarray(table, np.float64) - high.astype(np.float64)).astype(jnp.bfloat16)
    return high, low


def build_tables(side):
    plane = side * side
    half = plane // 2
    edge = side // 2
    ylo, zz = np.divmod(np.arange(half), side)
    scale = 1.0 / (2.2 * side**3)
    forward = np.zeros((2, 2, plane, plane))
    inverse = np.zeros((2, 2, plane, plane))
    tables = np.zeros((2, side // 2, 2, 8, half))
    packs = plane_sets(side)
    for parity in (0, 1):
        kyi, kz = np.divmod(np.arange(half), side)
        ky = 2 * kyi + parity
        order = window_order(parity, (ky == edge) | (kz == edge))
        ky, kz = ky[order], kz[order]
        angle = 2 * np.pi / side * ((np.outer(ylo, ky) + np.outer(zz, kz)) % side)
        c, s = np.cos(angle), np.sin(angle)
        forward[parity, 1] = np.block([[c, -s], [s, c]])
        inverse[parity, 1] = np.block([[c.T, s.T], [-s.T, c.T]]) * scale
        for kx in range(1, side // 2):
            tables[parity, kx, :, 0:3] = normal_at(np.full(half, kx), ky, kz, side)
            tables[parity, kx, :, 3:6] = normal_at(np.full(half, -kx), -ky, -kz, side)
            tables[parity, kx, :, 6] = 2.0
        columns = packs[parity]
        order = window_order(parity, (columns[:, 0] == edge) | (columns[:, 1] == edge))
        ky, kz, imag, single = columns[order].T
        angle = 2 * np.pi / side * ((np.outer(ylo, ky) + np.outer(zz, kz)) % side)
        fwd = np.where(imag[None], -np.sin(angle), np.cos(angle))
        share = np.where(single, 1.0, 2.0)
        inv = (fwd * share[None]).T * scale
        forward[parity, 0, :half, :half] = fwd
        forward[parity, 0, half:, half:] = fwd
        inverse[parity, 0, :half, :half] = inv
        inverse[parity, 0, half:, half:] = inv
        for part, kx in ((0, 0), (1, edge)):
            full = np.full(half, kx)
            tables[parity, 0, part, 0:3] = normal_at(full, ky, kz, side)
            tables[parity, 0, part, 3:6] = normal_at(-full, -ky, -kz, side)
            tables[parity, 0, part, 6] = share
    fh, fl = split_table(forward)
    ih, il = split_table(inverse)
    return np.stack([fh, fl]), np.stack([ih, il]), tables.astype(np.float32)


def real_transform(values):
    count = len(values)
    if count == 2:
        return [(values[0] + values[1], None), (values[0] - values[1], None)]
    even = real_transform(values[0::2])
    odd = real_transform(values[1::2])
    half = count // 2
    result = [None] * (half + 1)
    result[0] = (even[0][0] + odd[0][0], None)
    result[half] = (even[0][0] - odd[0][0], None)
    for k in range(1, half // 2):
        (er, ei), (orr, oi) = even[k], odd[k]
        angle = 2 * math.pi * k / count
        c, s = math.cos(angle), math.sin(angle)
        if abs(c - s) < 1e-9:
            tr, ti = (orr + oi) * c, (oi - orr) * c
        else:
            tr, ti = orr * c + oi * s, oi * c - orr * s
        result[k] = (er + tr, ei + ti)
        result[half - k] = (er - tr, ti - ei)
    result[half // 2] = (even[half // 2][0], -odd[half // 2][0])
    return result


def real_inverse(spectrum):
    half = len(spectrum) - 1
    count = 2 * half
    if count == 2:
        return [spectrum[0][0] + spectrum[1][0], spectrum[0][0] - spectrum[1][0]]
    even = [None] * (half // 2 + 1)
    odd = [None] * (half // 2 + 1)
    even[0] = (spectrum[0][0] + spectrum[half][0], None)
    odd[0] = (spectrum[0][0] - spectrum[half][0], None)
    for k in range(1, half // 2):
        (ar, ai), (br, bi) = spectrum[k], spectrum[half - k]
        even[k] = (ar + br, ai - bi)
        dr, di = ar - br, ai + bi
        angle = 2 * math.pi * k / count
        c, s = math.cos(angle), math.sin(angle)
        if abs(c - s) < 1e-9:
            odd[k] = ((dr - di) * c, (dr + di) * c)
        else:
            odd[k] = (dr * c - di * s, dr * s + di * c)
    mid_re, mid_im = spectrum[half // 2]
    even[half // 2] = (mid_re * 2.0, None)
    odd[half // 2] = (mid_im * -2.0, None)
    first, second = real_inverse(even), real_inverse(odd)
    result = []
    for a, b in zip(first, second):
        result += [a, b]
    return result


def potential(entries, normal):
    n0, n1, n2 = normal
    t0 = entries[0] * n0 + entries[5] * n1 + entries[4] * n2
    t1 = entries[5] * n0 + entries[1] * n1 + entries[3] * n2
    t2 = entries[4] * n0 + entries[3] * n1 + entries[2] * n2
    load = (n0 * t0 + n1 * t1 + n2 * t2) * (COUPLING * 1.1)
    return t0 - n0 * load, t1 - n1 * load, t2 - n2 * load


def strain_of(plus, minus, table):
    n0, n1, n2, m0, m1, m2 = table
    u0, u1, u2 = plus
    v0, v1, v2 = minus
    return (
        n0 * u0 + m0 * v0,
        n1 * u1 + m1 * v1,
        n2 * u2 + m2 * v2,
        (n1 * u2 + n2 * u1 + m1 * v2 + m2 * v1) * 0.5,
        (n0 * u2 + n2 * u0 + m0 * v2 + m2 * v0) * 0.5,
        (n0 * u1 + n1 * u0 + m0 * v1 + m1 * v0) * 0.5,
    )


def split_rows(value):
    high = value.astype(BF16)
    return high, (value - high.astype(F32)).astype(BF16)


def product(high, low, table_high, table_low):
    dot = functools.partial(jnp.dot, preferred_element_type=F32)
    return dot(high, table_high) + (dot(low, table_high) + dot(high, table_low))


def column_to_row(column, diagonal):
    return jnp.sum(jnp.where(diagonal, column, 0.0), axis=0, keepdims=True)


def row_to_column(row, diagonal):
    return jnp.sum(jnp.where(diagonal, row, 0.0), axis=1, keepdims=True)


def padded_row(ref):
    row = ref[...].astype(F32)
    return jnp.concatenate([row, jnp.zeros((1, LANES - row.shape[1]), F32)], axis=1)


def slot_choice(owner_ref, points, owners, dense):
    lane = lax.broadcasted_iota(jnp.int32, (points, LANES), 1)
    sub = lax.broadcasted_iota(jnp.int32, (points, LANES), 0)
    diagonal = lane == sub
    if not dense:
        return jnp.where(diagonal, 1.0, 0.0), lane
    owner_row = padded_row(owner_ref)
    owner_col = row_to_column(owner_row, diagonal)
    earlier = jnp.where((owner_col == owner_row) & (lane < sub), 1.0, 0.0)
    rank_col = jnp.sum(earlier, axis=1, keepdims=True)
    slot_row = column_to_row(rank_col * owners + owner_col, diagonal)
    return jnp.where((slot_row == sub.astype(F32)) & (lane < points), 1.0, 0.0), lane


def forward_groups(dims, groups, tau, high, low):
    side, slabs = dims

    def step(g, carry):
        at = pl.ds(pl.multiple_of(g * 16, 16), 16)
        for parity in (0, 1):
            values = []
            for x in range(side):
                a, b = tau[2 * x, at], tau[2 * x + 1, at]
                values.append(a + b if parity == 0 else a - b)
            out = real_transform(values)
            for s in range(slabs):
                re, im = out[s] if s else (out[0][0], out[slabs][0])
                for k, v in ((0, re), (1, im)):
                    hi, lo = split_rows(v)
                    high[parity, s, at, k * LANES : (k + 1) * LANES] = hi
                    low[parity, s, at, k * LANES : (k + 1) * LANES] = lo
        return carry

    lax.fori_loop(0, groups, step, 0)


def multiply(high, low, table, spec, done=None):
    slabs, rows, plane = high.shape[1:]
    for parity in (0, 1):
        spec[parity, 0] = product(
            high[parity, 0], low[parity, 0], table[0, parity, 0], table[1, parity, 0]
        )
        spec[parity, 1:] = product(
            high[parity, 1:].reshape((slabs - 1) * rows, plane),
            low[parity, 1:].reshape((slabs - 1) * rows, plane),
            table[0, parity, 1], table[1, parity, 1],
        ).reshape(slabs - 1, rows, plane)
        if done is not None:
            done(parity)


def inverse_rows(spec, at, slabs, emit):
    for yhi in (0, 1):
        parts = []
        for s in range(slabs):
            both = []
            for k in (0, 1):
                lanes = slice(k * LANES, (k + 1) * LANES)
                e, o = spec[0, s, at, lanes], spec[1, s, at, lanes]
                both.append(e + o if yhi == 0 else e - o)
            parts.append(both)
        spectrum = [(parts[0][0], None)] + [tuple(b) for b in parts[1:]]
        spectrum.append((parts[0][1], None))
        for x, v in enumerate(real_inverse(spectrum)):
            emit(2 * x + yhi, v)


def first_kernel(
    dims, owner_ref, warm_hbm, moduli_hbm, forward_hbm,
    spec_hbm, both_hbm, mean_ref,
    forward, warm, moduli, spec, tau, high, low, sems,
):
    points, comps, side, owners, dense = dims
    tiles = side**3 // LANES
    parts = 4
    span = side**3 // parts
    stride = moduli.shape[0] // points
    moduli_copies = [
        pltpu.make_async_copy(
            moduli_hbm.at[g], moduli.at[pl.ds(g * stride, 2 * tiles)], sems.at[0]
        )
        for g in range(points)
    ]
    warm_copies = [
        pltpu.make_async_copy(
            warm_hbm.at[:, :, pl.ds(q * span, span)], warm.at[:, :, pl.ds(q * span, span)],
            sems.at[1 + q],
        )
        for q in range(parts)
    ]
    table_copy = pltpu.make_async_copy(forward_hbm, forward, sems.at[1 + parts])
    for copy in moduli_copies + warm_copies + [table_copy]:
        copy.start()
    octets = points // 8
    choose, lane = slot_choice(owner_ref, points, owners, dense)
    pick = jnp.sum(choose * lane.astype(F32), axis=1, keepdims=True).astype(jnp.int32)
    picks = [jnp.broadcast_to(pick[8 * o : 8 * o + 8], (8, LANES)) for o in range(octets)]
    locals_ = [
        [jnp.clip(picks[o] - 8 * source, 0, 7) for source in range(octets)] for o in range(octets)
    ]
    beyond = [[picks[o] >= 8 * source for source in range(octets)] for o in range(octets)]

    def gather(value):
        if not dense:
            return value
        outs = []
        for o in range(octets):
            best = None
            for source in range(octets):
                got = jnp.take_along_axis(
                    value[8 * source : 8 * source + 8], locals_[o][source], axis=0,
                    mode="promise_in_bounds",
                )
                best = got if best is None else jnp.where(beyond[o][source], got, best)
            outs.append(best)
        return jnp.concatenate(outs, axis=0)

    def load_step(t, sums):
        at = pl.ds(pl.multiple_of(t * LANES, LANES), LANES)
        pair = [
            gather(
                jnp.concatenate(
                    [
                        moduli[pl.ds(8 * o * stride + 2 * t + i, 8, stride=stride), :]
                        for o in range(octets)
                    ],
                    axis=0,
                )
            )
            for i in (0, 1)
        ]
        lamb = pair[0] - REF_MODULUS
        mu = pair[1] * 2.0 - 2.0 * REF_MODULUS
        eps = [gather(warm[c, :, at]) for c in range(comps)]
        extra = lamb * (eps[0] + eps[1] + eps[2])
        for c in range(comps):
            value = mu * eps[c]
            tau[t, c * points : (c + 1) * points] = value + extra if c < 3 else value
        tau[t, comps * points : (comps + 1) * points] = lamb
        tau[t, (comps + 1) * points :] = mu
        return tuple(s + e for s, e in zip(sums, eps + [lamb, mu]))

    zero = jnp.zeros((points, LANES), F32)
    sums = (zero,) * (comps + 2)
    for copy in moduli_copies:
        copy.wait()
    for q in range(parts):
        warm_copies[q].wait()
        sums = lax.fori_loop(q * tiles // parts, (q + 1) * tiles // parts, load_step, sums)
    both_copy = pltpu.make_async_copy(
        tau.at[:, pl.ds(comps * points, 2 * points)], both_hbm, sems.at[0]
    )
    both_copy.start()
    for c in range(comps + 2):
        mean_ref[c * points : (c + 1) * points] = jnp.broadcast_to(
            jnp.sum(sums[c], axis=1, keepdims=True) * (1.0 / side**3), (points, LANES)
        )
    forward_groups((side, side // 2), (comps + 2) * points // 16, tau, high, low)
    table_copy.wait()
    out_copies = []

    def done(parity):
        copy = pltpu.make_async_copy(spec.at[parity], spec_hbm.at[parity], sems.at[1 + parity])
        copy.start()
        out_copies.append(copy)

    multiply(high, low, forward, spec, done)
    both_copy.wait()
    for copy in out_copies:
        copy.wait()


def second_kernel(
    dims,
    part_ref, owner_ref, sweeps_ref, weight_ref, conn_ref, grads_ref, table_ref, mean_ref,
    normals_ref, first_hbm, both_hbm, forward_hbm, inverse_hbm,
    send_ref, stress_ref, force_ref,
    first_ref, both, forward, inverse, tau, high, low, spec, pot, edge, full, macro_buf, loads_buf,
    sems, slab_sems,
):
    points, comps, side, devices, node_dev, halo, row_span, nodes_part, owners, dense = dims
    copies = [
        pltpu.make_async_copy(inverse_hbm, inverse, sems.at[0]),
        pltpu.make_async_copy(both_hbm, both, sems.at[1]),
        pltpu.make_async_copy(forward_hbm, forward, sems.at[2]),
    ]

    def slab_copy(s):
        return pltpu.make_async_copy(
            first_hbm.at[:, pl.ds(s, 1)], first_ref.at[:, pl.ds(s, 1)], slab_sems.at[s]
        )

    for s in range(side // 2):
        slab_copy(s).start()
    for copy in copies:
        copy.start()
    voxels = side**3
    tiles = voxels // LANES
    slabs = side // 2
    part = part_ref[0]
    choose, _ = slot_choice(owner_ref, points, owners, dense)
    count_col = jnp.sum(choose * padded_row(sweeps_ref), axis=1, keepdims=True)
    weight_row = padded_row(weight_ref)

    exch = table_ref[...]
    dev_sub = lax.broadcasted_iota(jnp.int32, exch.shape, 0)
    below = jnp.sum(jnp.where(dev_sub == (part - 1) * row_span, exch, 0.0), axis=0, keepdims=True)
    above = jnp.sum(jnp.where(dev_sub == (part + 1) * row_span, exch, 0.0), axis=0, keepdims=True)
    parts = devices // row_span
    wide = table_ref.shape[1]
    elane = lax.broadcasted_iota(jnp.int32, (1, wide), 1)
    lane_f = elane.astype(F32)
    part_f = part.astype(F32)
    span = float(nodes_part)
    low_id = jnp.where(part > 0, below + (part_f - 1.0) * span, -1.0)
    high_id = jnp.where(part < parts - 1, above + (part_f + 1.0) * span, -1.0)
    node_row = jnp.where(
        elane < nodes_part,
        part_f * span + lane_f,
        jnp.where(elane < nodes_part + halo, low_id, high_id),
    )
    corner = lax.broadcasted_iota(jnp.int32, (8, LANES), 0)
    corner_lane = lax.broadcasted_iota(jnp.int32, (8, LANES), 1)
    link_rows = conn_ref[...].astype(F32)
    link_rows = jnp.concatenate(
        [link_rows, jnp.zeros((link_rows.shape[0], LANES - 8), F32)], axis=1
    )
    links = jnp.concatenate(
        [row_to_column(link_rows[e : e + 1], corner == corner_lane) for e in range(points // 8)],
        axis=0,
    )
    node_col = jnp.sum(jnp.where(links == lane_f, node_row, 0.0), axis=1, keepdims=True)
    device_col = jnp.floor(node_col * (1.0 / node_dev))
    inner_col = node_col - device_col * node_dev
    nlinks = links.shape[0]
    hit_lane = lax.broadcasted_iota(jnp.int32, (nlinks, devices), 1).astype(F32)
    hit = jnp.where(hit_lane == device_col, 1.0, 0.0)
    flat_lane = lax.broadcasted_iota(jnp.int32, (nlinks, LANES), 1)
    group = flat_lane // node_dev
    inside = jnp.where(
        ((flat_lane - group * node_dev).astype(F32) == inner_col) & (group < 3), 1.0, 0.0
    )
    fetched = jnp.dot(hit, exch[:, :LANES], preferred_element_type=F32,
                      precision=lax.Precision.HIGHEST) * inside
    moved = [
        jnp.sum(jnp.where(group == i, fetched, 0.0), axis=1, keepdims=True) for i in range(3)
    ]
    elements = points // 8
    glane = lax.broadcasted_iota(jnp.int32, (8, LANES), 1)
    spread = []
    for i in range(3):
        acc = jnp.zeros((8, LANES), F32)
        for e in range(elements):
            acc = jnp.where(glane // 8 == e, moved[i][8 * e : 8 * e + 8], acc)
        spread.append(acc)
    grads = [
        jnp.concatenate([grads_ref[j], jnp.zeros((8, LANES - points), F32)], axis=1)
        for j in range(3)
    ]
    grad = [
        [jnp.sum(spread[i] * grads[j], axis=0, keepdims=True) for j in range(3)] for i in range(3)
    ]
    macro_rows = [grad[0][0], grad[1][1], grad[2][2]] + [
        (grad[a][b] + grad[b][a]) * 0.5 for a, b in PAIRS[3:]
    ]
    macro_cols = [jnp.sum(choose * row, axis=1, keepdims=True) for row in macro_rows]


    octets = points // 8
    shift = [
        jnp.broadcast_to(macro_cols[c], (points, LANES)) - mean_ref[c * points : (c + 1) * points]
        for c in range(comps)
    ]
    shift_trace = shift[0] + shift[1] + shift[2]
    macro = [jnp.broadcast_to(col, (points, LANES)) for col in macro_cols]
    again = jnp.broadcast_to(count_col > 1.0, (points, LANES))
    block = send_ref.shape[0] // points

    def send(o, index, value):
        if dense:
            per_owner = points // owners
            send_ref[pl.ds(o * block + index, owners, stride=per_owner * block), :] = value
        else:
            send_ref[pl.ds(8 * o * block + index, 8, stride=block), :] = value

    edge_base = 3 * 4 * slabs
    window_rows = slabs * 2 * WINDOW // LANES
    at_window = lax.broadcasted_iota(jnp.int32, (8, LANES), 1)

    def green_stage(last):
        def load(parity, s, k, o):
            lanes = slice(k * LANES, (k + 1) * LANES)
            if last:
                return [
                    spec[parity, s, c * points + 8 * o : c * points + 8 * o + 8, lanes]
                    for c in range(comps)
                ]
            rows = slice(8 * o, 8 * o + 8)
            raw = [
                first_ref[parity, s, c * points + 8 * o : c * points + 8 * o + 8, lanes]
                for c in range(comps + 2)
            ]
            extra = raw[comps] * shift_trace[rows]
            entries = [raw[c] + raw[comps + 1] * shift[c][rows] for c in range(comps)]
            return [entries[c] + extra if c < 3 else entries[c] for c in range(comps)]

        def step(s, acc):
            acc = list(acc)
            if not last:
                slab_copy(s).wait()
            for k in (0, 1):
                lanes = slice(k * LANES, (k + 1) * LANES)
                results = [[[] for _ in range(comps)] for _ in (0, 1)]
                edges = [[None, None] for _ in range(octets)]
                for parity in (0, 1):
                    table = [
                        jnp.broadcast_to(normals_ref[parity, s, k, d : d + 1, :], (8, LANES))
                        for d in range(7)
                    ]
                    for o in range(octets):
                        rows = slice(8 * o, 8 * o + 8)
                        entries = load(parity, s, k, o)
                        plus = potential(entries, table[0:3])
                        minus = potential(entries, table[3:6])
                        strains = strain_of(plus, minus, table[0:6])
                        for c in range(comps):
                            results[parity][c].append(strains[c])
                        share_l = table[6] * first_ref[
                            parity, s, comps * points + 8 * o : comps * points + 8 * o + 8, lanes
                        ]
                        share_m = table[6] * first_ref[
                            parity, s,
                            (comps + 1) * points + 8 * o : (comps + 1) * points + 8 * o + 8, lanes,
                        ]
                        base = o * (comps + 1)
                        acc[base] = acc[base] + share_l * (strains[0] + strains[1] + strains[2])
                        for c in range(comps):
                            acc[base + 1 + c] = acc[base + 1 + c] + share_m * strains[c]
                        edges[o][parity] = minus
                        for d in range(3):
                            index = (d * 2 + parity) * slabs * 2 + s * 2 + k
                            if last:
                                kept = pot[o, index]
                                send(o, index, jnp.where(again[rows], plus[d], kept))
                            else:
                                pot[o, index] = plus[d]
                if not last:
                    for parity in (0, 1):
                        for c in range(comps):
                            hi, lo = split_rows(jnp.concatenate(results[parity][c], axis=0))
                            high[parity, s, c * points : (c + 1) * points, lanes] = hi
                            low[parity, s, c * points : (c + 1) * points, lanes] = lo
                for o in range(octets):
                    for d in range(3):
                        joined = jnp.where(
                            at_window < SPLIT, edges[o][0][d], edges[o][1][d]
                        )
                        edge[o, d, s * 2 + k] = (
                            jnp.where(again[8 * o : 8 * o + 8], joined, edge[o, d, s * 2 + k])
                            if last else joined
                        )
                        if k == 1:
                            @pl.when(s == 0)
                            def _():
                                for parity in (0, 1):
                                    value = edges[o][parity][d]
                                    if last:
                                        value = jnp.where(
                                            again[8 * o : 8 * o + 8], value, full[o, d, parity]
                                        )
                                    full[o, d, parity] = value
            return tuple(acc)

        zero = jnp.zeros((8, LANES), F32)
        return lax.fori_loop(0, slabs, step, (zero,) * (octets * (comps + 1)))

    first = green_stage(False)
    copies[0].wait()
    multiply(high, low, inverse, spec)

    def field_step(c, carry):
        at = pl.ds(pl.multiple_of(c * points, points), points)
        base = macro_buf[c]

        def emit(tile, value):
            tau[tile, at] = base - value

        inverse_rows(spec, at, slabs, emit)
        return carry

    for c in range(comps):
        macro_buf[c] = macro[c]
    lax.fori_loop(0, comps, field_step, 0)
    copies[1].wait()

    def tau_step(t, carry):
        eps = [tau[t, c * points : (c + 1) * points] for c in range(comps)]
        extra = both[t, :points] * (eps[0] + eps[1] + eps[2])
        mu = both[t, points:]
        for c in range(comps):
            value = mu * eps[c]
            tau[t, c * points : (c + 1) * points] = value + extra if c < 3 else value
        return carry

    lax.fori_loop(0, tiles, tau_step, 0)
    forward_groups((side, slabs), comps * points // 16, tau, high, low)
    copies[2].wait()
    multiply(high, low, forward, spec)
    second = green_stage(True)

    row_lane = lax.broadcasted_iota(jnp.int32, (8, LANES), 1)
    per_row = LANES // WINDOW
    for o in range(octets):
        for d in range(3):
            for v in range(2 * slabs // per_row):
                value = edge[o, d, v * per_row]
                for q in range(1, per_row):
                    moved_q = pltpu.roll(edge[o, d, v * per_row + q], q * WINDOW, 1)
                    value = jnp.where(row_lane >= q * WINDOW, moved_q, value)
                send(o, edge_base + d * (2 * slabs // per_row) + v, value)
            for parity in (0, 1):
                send(o, edge_base + 3 * window_rows + d * 2 + parity, full[o, d, parity])
        value = jnp.zeros((8, LANES), F32)
        for c in range(comps):
            value = jnp.where(row_lane == c, macro[c][8 * o : 8 * o + 8], value)
        send(o, edge_base + 3 * window_rows + 6, value)

    sums = []
    for q in range(comps + 1):
        rows = [
            jnp.where(
                again[8 * o : 8 * o + 8], second[o * (comps + 1) + q], first[o * (comps + 1) + q]
            )
            for o in range(octets)
        ]
        sums.append(
            jnp.sum(jnp.concatenate(rows, axis=0), axis=1, keepdims=True)
            * (1.0 / (2.2 * float(voxels) * float(voxels)))
        )
    lamb_mean = mean_ref[comps * points : (comps + 1) * points]
    mu_mean = mean_ref[(comps + 1) * points :]
    trace = macro[0] + macro[1] + macro[2]
    bulk = (lamb_mean + REF_MODULUS) * trace - sums[0]
    stress_rows = []
    for c in range(comps):
        value = (mu_mean + 2.0 * REF_MODULUS) * macro[c] - sums[1 + c]
        if c < 3:
            value = value + bulk
        stress_rows.append(jnp.sum(choose * value, axis=0, keepdims=True))
    for c in range(comps):
        stress_ref[c : c + 1, :] = stress_rows[c]

    index_of = ((0, 5, 4), (5, 1, 3), (4, 3, 2))
    weighted = [row * weight_row for row in stress_rows]
    loads = jnp.zeros((nlinks, LANES), F32)
    for i in range(3):
        total = sum(grads[j] * weighted[index_of[i][j]] for j in range(3))
        columns = [
            jnp.sum(jnp.where(glane // 8 == e, total, 0.0), axis=1, keepdims=True)
            for e in range(elements)
        ]
        loads = jnp.where(group == i, jnp.concatenate(columns, axis=0), loads)
    loads = loads * inside
    force = lax.dot_general(
        hit, loads, (((0,), (0,)), ((), ())), preferred_element_type=F32,
        precision=lax.Precision.HIGHEST,
    )
    force_ref[...] = force
    last_row = edge_base + 3 * window_rows + 7
    for o in range(octets):
        send(o, last_row, jnp.zeros((8, LANES), F32))
    if dense:
        loads_buf[...] = jnp.zeros_like(loads_buf)
        loads_buf[row_span : row_span + devices] = force
        near = [
            loads_buf[pl.ds(pl.multiple_of((part + i) * row_span, row_span), row_span), :]
            for i in range(3)
        ]
        send(
            0, last_row,
            near[1] + pltpu.roll(near[0], PREV_LANE, 1) + pltpu.roll(near[2], NEXT_LANE, 1),
        )


def third_kernel(
    dims, recv_ref, normals_ref, inverse_hbm, out_ref, inverse, high, low, spec, sem
):
    points, comps, side = dims
    copy = pltpu.make_async_copy(inverse_hbm, inverse, sem)
    copy.start()
    slabs = side // 2
    block = recv_ref.shape[0] // points
    edge_base = 3 * 4 * slabs
    per_row = LANES // WINDOW
    window_rows = 2 * slabs // per_row
    octets = points // 8
    lane = lax.broadcasted_iota(jnp.int32, (8, LANES), 1)

    def fetch(o, index):
        return recv_ref[pl.ds(8 * o * block + index, 8, stride=block), :]

    for s in range(slabs):
        for k in (0, 1):
            window = s * 2 + k
            lanes = slice(k * LANES, (k + 1) * LANES)
            edges = []
            for o in range(octets):
                row = []
                for d in range(3):
                    value = fetch(o, edge_base + d * window_rows + window // per_row)
                    turn = (window % per_row) * WINDOW
                    row.append(pltpu.roll(value, LANES - turn, 1) if turn else value)
                edges.append(row)
            for parity in (0, 1):
                table = [
                    jnp.broadcast_to(normals_ref[parity, s, k, d : d + 1, :], (8, LANES))
                    for d in range(6)
                ]
                if parity == 0:
                    inside = lane < SPLIT
                else:
                    inside = (lane >= SPLIT) & (lane < WINDOW)
                results = [[] for _ in range(comps)]
                for o in range(octets):
                    plus = [
                        fetch(o, (d * 2 + parity) * slabs * 2 + window) for d in range(3)
                    ]
                    if s == 0 and k == 1:
                        minus = [
                            fetch(o, edge_base + 3 * window_rows + d * 2 + parity)
                            for d in range(3)
                        ]
                    else:
                        minus = [jnp.where(inside, edges[o][d], -plus[d]) for d in range(3)]
                    strains = strain_of(plus, minus, table)
                    for c in range(comps):
                        results[c].append(strains[c])
                for c in range(comps):
                    hi, lo = split_rows(jnp.concatenate(results[c], axis=0))
                    high[parity, s, c * points : (c + 1) * points, lanes] = hi
                    low[parity, s, c * points : (c + 1) * points, lanes] = lo
    copy.wait()
    multiply(high, low, inverse, spec)
    tops = [fetch(o, edge_base + 3 * window_rows + 6) for o in range(octets)]
    for c in range(comps):
        base = jnp.concatenate(
            [jnp.broadcast_to(top[:, c : c + 1], (8, LANES)) for top in tops], axis=0
        )

        def emit(tile, value):
            out_ref[c, :, tile * LANES : (tile + 1) * LANES] = base - value

        inverse_rows(spec, slice(c * points, (c + 1) * points), slabs, emit)


def pack_kernel(dims, displacement_ref, halo_ref, out_ref):
    nodes_part, halo = dims
    moved = displacement_ref[...]
    halo_f = halo_ref[...].astype(F32)
    node_dev = moved.shape[1]
    wide = out_ref.shape[1]
    pieces = [moved[0:1], moved[1:2], moved[2:3]]
    pieces.append(jnp.zeros((1, nodes_part - 3 * node_dev), F32))
    pieces += [halo_f[1:2], halo_f[0:1]]
    pieces.append(jnp.zeros((1, wide - nodes_part - 2 * halo), F32))
    out_ref[...] = jnp.broadcast_to(jnp.concatenate(pieces, axis=1), out_ref.shape)


def on_device(
    displacement, shape_grads, point_weights, conn, halo_nodes, warm_strain, moduli, owner, sweeps
):
    axes = ("mesh", "rve")
    points, comps, voxels = warm_strain.shape
    side = round(voxels ** (1.0 / 3.0))
    tiles = voxels // LANES
    slabs = side // 2
    plane = side * side
    owners = lax.axis_size("rve")
    devices = lax.axis_size("mesh") * owners
    node_dev = displacement.shape[1]
    nodes_part = node_dev * owners
    halo = halo_nodes.shape[1]
    per_owner = max(2, points // owners)
    dense = per_owner * owners == points and owners == 8
    wide = -(-(nodes_part + 2 * halo) // LANES) * LANES
    vmem = pl.BlockSpec(memory_space=pltpu.VMEM)
    hbm = pl.BlockSpec(memory_space=pltpu.HBM)
    params = pltpu.CompilerParams(vmem_limit_bytes=63 << 20)

    packed = pl.pallas_call(
        functools.partial(pack_kernel, (nodes_part, halo)),
        out_shape=jax.ShapeDtypeStruct((devices, wide), F32),
        in_specs=[vmem, vmem],
        out_specs=vmem,
        name="pack",
    )(displacement, halo_nodes)
    table = lax.all_to_all(packed, axes, split_axis=0, concat_axis=0, tiled=True)

    owner_row = owner.reshape(1, points)
    sweeps_row = sweeps.reshape(1, points)
    weight_row = point_weights.reshape(1, points)
    part = lax.axis_index("mesh").astype(jnp.int32).reshape(1)
    warm = warm_strain.transpose(1, 0, 2)
    moduli_rows = (
        moduli.reshape(points, 2, tiles, LANES).transpose(0, 2, 1, 3).reshape(points, -1, LANES)
    )
    forward, inverse, normals = (jnp.asarray(t) for t in build_tables(side))
    rows = comps * points
    more = (comps + 2) * points
    octets = points // 8
    table_scratch = pltpu.VMEM(forward.shape, BF16)
    spec, both, mean = pl.pallas_call(
        functools.partial(first_kernel, (points, comps, side, owners, dense)),
        out_shape=(
            jax.ShapeDtypeStruct((2, slabs, more, plane), F32),
            jax.ShapeDtypeStruct((tiles, 2 * points, LANES), F32),
            jax.ShapeDtypeStruct((more, LANES), F32),
        ),
        in_specs=[vmem, hbm, hbm, hbm],
        out_specs=(hbm, hbm, vmem),
        scratch_shapes=[
            table_scratch,
            pltpu.VMEM((comps, points, voxels), F32),
            pltpu.VMEM((points * (2 * tiles + 8), LANES), F32),
            pltpu.VMEM((2, slabs, more, plane), F32),
            pltpu.VMEM((tiles, more, LANES), F32),
            pltpu.VMEM((2, slabs, more, plane), BF16),
            pltpu.VMEM((2, slabs, more, plane), BF16),
            pltpu.SemaphoreType.DMA((6,)),
        ],
        compiler_params=params,
        cost_estimate=pl.CostEstimate(
            flops=2 * 3 * 16 * more * plane * plane, transcendentals=0, bytes_accessed=4 << 20
        ),
        name="first",
    )(owner_row, warm, moduli_rows, forward)

    dims = (points, comps, side, devices, node_dev, halo, owners, nodes_part, owners, dense)
    block = 3 * 4 * slabs + 3 * (2 * slabs * WINDOW // LANES) + 8
    send, stress, force = pl.pallas_call(
        functools.partial(second_kernel, dims),
        out_shape=(
            jax.ShapeDtypeStruct((points * block, LANES), F32),
            jax.ShapeDtypeStruct((8, LANES), F32),
            jax.ShapeDtypeStruct((devices, LANES), F32),
        ),
        in_specs=[pl.BlockSpec(memory_space=pltpu.SMEM)] + [vmem] * 8 + [hbm] * 4,
        out_specs=(vmem,) * 3,
        scratch_shapes=[
            pltpu.VMEM((2, slabs, more, plane), F32),
            pltpu.VMEM((tiles, 2 * points, LANES), F32),
            table_scratch,
            table_scratch,
            pltpu.VMEM((tiles, rows, LANES), F32),
            pltpu.VMEM((2, slabs, rows, plane), BF16),
            pltpu.VMEM((2, slabs, rows, plane), BF16),
            pltpu.VMEM((2, slabs, rows, plane), F32),
            pltpu.VMEM((octets, 3 * 4 * slabs, 8, LANES), F32),
            pltpu.VMEM((octets, 3, 2 * slabs, 8, LANES), F32),
            pltpu.VMEM((octets, 3, 2, 8, LANES), F32),
            pltpu.VMEM((comps, points, LANES), F32),
            pltpu.VMEM((devices + 2 * owners, LANES), F32),
            pltpu.SemaphoreType.DMA((3,)),
            pltpu.SemaphoreType.DMA((slabs,)),
        ],
        compiler_params=params,
        cost_estimate=pl.CostEstimate(
            flops=2 * 2 * 3 * 16 * rows * plane * plane, transcendentals=0, bytes_accessed=6 << 20
        ),
        name="second",
    )(
        part, owner_row, sweeps_row, weight_row, conn.T, shape_grads, table, mean, normals,
        spec, both, forward, inverse,
    )

    finish = pl.pallas_call(
        functools.partial(third_kernel, (points, comps, side)),
        out_shape=jax.ShapeDtypeStruct((comps, points, voxels), F32),
        in_specs=[vmem, vmem, hbm],
        out_specs=vmem,
        scratch_shapes=[
            table_scratch,
            pltpu.VMEM((2, slabs, rows, plane), BF16),
            pltpu.VMEM((2, slabs, rows, plane), BF16),
            pltpu.VMEM((2, slabs, rows, plane), F32),
            pltpu.SemaphoreType.DMA,
        ],
        compiler_params=pltpu.CompilerParams(vmem_limit_bytes=24 << 20),
        cost_estimate=pl.CostEstimate(
            flops=2 * 3 * 16 * rows * plane * plane, transcendentals=0, bytes_accessed=4 << 20
        ),
        name="third",
    )
    comps_out = stress[:comps, :points]
    if dense:
        received = lax.all_to_all(
            send.reshape(owners, per_owner * block, LANES), "rve",
            split_axis=0, concat_axis=0, tiled=True,
        ).reshape(points * block, LANES)
        micro = finish(received, normals, inverse).transpose(1, 0, 2)
        found = received.reshape(owners, per_owner * block, LANES)[:, block - 1]
        found = jnp.sum(found, axis=0)
        parts = lax.axis_size("mesh")
        up = lax.ppermute(found, "mesh", [(i, i + 1) for i in range(parts - 1)])
        down = lax.ppermute(found, "mesh", [(i + 1, i) for i in range(parts - 1)])
        count = 3 * node_dev
        nodal = (
            found[:count] + up[NEXT_LANE : NEXT_LANE + count] + down[PREV_LANE : PREV_LANE + count]
        ).reshape(3, node_dev)
    else:
        slots = owners * per_owner
        final = finish(send, normals, inverse).transpose(1, 0, 2)
        order = jnp.arange(points, dtype=jnp.int32)
        same = owner[:, None] == owner[None, :]
        rank = jnp.sum((same & (order[None, :] < order[:, None])).astype(jnp.int32), axis=1)
        slot = owner * per_owner + rank
        fields = jnp.zeros((slots, comps, voxels), F32).at[slot].set(final)
        flags = jnp.zeros((slots,), F32).at[slot].set(1.0)
        fields = lax.all_to_all(fields, "rve", split_axis=0, concat_axis=0, tiled=True)
        flags = lax.all_to_all(flags, "rve", split_axis=0, concat_axis=0, tiled=True)
        filled = jnp.nonzero(flags > 0.5, size=points)[0].astype(jnp.int32)
        micro = fields[filled]
        pieces = lax.all_to_all(force, axes, split_axis=0, concat_axis=0, tiled=True)
        nodal = jnp.sum(pieces, axis=0)[: 3 * node_dev].reshape(3, node_dev)
    return (nodal, comps_out, micro)


def solution(mesh):
    both = ("mesh", "rve")
    in_specs = (
        P(None, both), P(None, None, both), P(both), P(None, both), P(None, "mesh"),
        P(both, None, None), P(both, None, None), P(both), P(both),
    )
    out_specs = (P(None, both), P(None, both), P(both, None, None))

    return jax.shard_map(
        on_device, mesh=mesh, in_specs=in_specs, out_specs=out_specs, check_vma=False
    )
```

time: 71.1 us -> 54.4 us (0.77)
  waiting for transfers between devices: 23.7 us -> 0.56 us
  blocking collectives: 9.31 us -> 17.9 us
  local copies, waits for them, and re-layouts: 8.29 us -> 1.28 us
  Pallas kernels: 15.4 us -> 20.4 us
  starting transfers between devices: 10.9 us -> 13.2 us
  other arithmetic: 2.26 us -> 0.1 us
    all_to_all x2 -> x1, waiting for transfers between devices: 23.7 us -> 0.55 us  [on_device(): lax.all_to_all(packed, axes, split_axis=0, concat_axis=0, tiled=True)]
    all_to_all x1, blocking collectives: 9.31 us -> 17.9 us  [on_device(): lax.all_to_all(send.reshape(owners, per_owner * block, LANES), 'rve', spl...]
    ppermute x0 -> x2, starting transfers between devices: none -> 5.83 us  [the longest x1 4.55 us: on_device(): up = lax.ppermute(found, 'mesh', [(i, i + 1) for i in range(parts - 1)])]
    pallas_call x2 -> x4, Pallas kernels: 15.4 us -> 20.4 us  [the longest x1 9.53 us: on_device(): pl.pallas_call(functools.partial(second_kernel, dims), out_shape=(jax.Sha...]
    all_to_all x2 -> x1, starting transfers between devices: 10.9 us -> 7.33 us  [on_device(): lax.all_to_all(packed, axes, split_axis=0, concat_axis=0, tiled=True)]
    unnamed x16 -> x6, local copies, waits for them, and re-layouts: 3.15 us -> 0.61 us
    slice x1 -> x0, local copies, waits for them, and re-layouts: 1.77 us -> none  [on_device(): lame, shear = (moduli[:, 0], moduli[:, 1])]
    scatter x2 -> x0, other arithmetic: 1.52 us -> none  [the longest x1 0.76 us: on_device(): row = row.at[nodes_part:nodes_part + halo].set(halo_nodes[1].astype(F32))]
  transfers between devices with their start and end apart: 2 -> 3, of which waited for: 2 -> 1; matrix products, arithmetic and copies ran while one was open for 6% -> 0% of each run, Pallas kernels for 0% -> 18%
where the time goes in v1:
time: 54.4 us; the launch traced here: 54.1 us
  Pallas kernels  20.4 us (38%)
  blocking collectives  17.9 us (33%)
  starting transfers between devices  13.2 us (24%)
  local copies, waits for them, and re-layouts  1.28 us (2%)
  between operations  0.73 us (1%)
  waiting for transfers between devices  0.56 us (1%)
    all_to_all x1, blocking collectives, on_device(): lax.all_to_all(send.reshape(owners, per_owner * block, LANES), 'rve', spl...  17.9 us
    pallas_call x1, Pallas kernels, on_device(): pl.pallas_call(functools.partial(second_kernel, dims), out_shape=(jax.Sha...  9.53 us
    all_to_all x1, starting transfers between devices, on_device(): lax.all_to_all(packed, axes, split_axis=0, concat_axis=0, tiled=True)  7.33 us
    pallas_call x1, Pallas kernels, on_device(): pl.pallas_call(functools.partial(first_kernel, (points, comps, side, owne...  6.54 us
    ppermute x1, starting transfers between devices, on_device(): up = lax.ppermute(found, 'mesh', [(i, i + 1) for i in range(parts - 1)])  4.55 us
    pallas_call x1, Pallas kernels, on_device(): micro = finish(received, normals, inverse).transpose(1, 0, 2)  2.98 us
    pallas_call x1, Pallas kernels, on_device(): pl.pallas_call(functools.partial(pack_kernel, (nodes_part, halo)), out_sh...  1.38 us
    ppermute x1, starting transfers between devices, on_device(): down = lax.ppermute(found, 'mesh', [(i + 1, i) for i in range(parts - 1)])  1.28 us
  transfers between devices with their start and end apart: 3, of which 1 were waited for; matrix products, arithmetic and copies ran while one was open for 0% of the time, Pallas kernels for 18%

profile of v1, /device:TPU:0, one launch (start us, length us, event | category | flops | bytes accessed | tf_op | source)
XLA Modules:
  0.0 54.1 jit_solution(17854090850783084777)
XLA Ops:
  0.6 1.4 %pack.1 = f32[32,128]{1,0:T(8,128)} custom-call(f32[3,4]{1,0:T(4,128)} %displacement_ref.1, s32[2,8]{1,0:T(2,128)} %halo_ref.1), custom_call_target="tpu_custom_call" | custom-call | tf_op jit(solution)/shard_map/pack/pallas_call | solution.py:801
  2.0 7.3 %all-to-all-start = ((f32[32,1,128]{2,1,0:T(1,128)}), f32[32,1,128]{2,1,0:T(1,128)S(1)}, u32[]{:S(2)}, u32[]{:S(2)}) async-start(f32[32,1,128]{2,1,0:T(1,128)} %bitcast.25), calls=%async_computation | async-start | bytes 32768 | tf_op jit(solution)/shard_map/all_to_all | solution.py:808
  9.3 6.5 %first.1 = (f32[2,8,128,256]{3,2,1,0:T(8,128)}, f32[32,32,128]{2,1,0:T(8,128)}, f32[128,128]{1,0:T(8,128)}) custom-call(s32[1,16]{1,0:T(1,128)} %bitcast.26, f32[6,16,4096]{2,1,0:T(8,128)} %bitcast.21, f32[16,64,128]{2,1,0:T(8,128)} %bitcast.23, bf16[2,2,2,256,256]{4,3,2,1,0:T(8,128)(2,1)} %constant.13.clone.forward_hbm), custom_call_target="tpu_custom_call" | custom-call | flops 805306368 | bytes 4194304 | tf_op jit(solution)/shard_map/first/pallas_call | solution.py:823
  15.9 0.6 %all-to-all-done = f32[32,1,128]{2,1,0:T(1,128)S(1)} async-done(((f32[32,1,128]{2,1,0:T(1,128)}), f32[32,1,128]{2,1,0:T(1,128)S(1)}, u32[]{:S(2)}, u32[]{:S(2)}) %all-to-all-start) | async-done | bytes 16416 | tf_op jit(solution)/shard_map/all_to_all | solution.py:808
  16.4 0.0 copy-start.2
  16.4 0.6 %copy-done.2 = f32[32,1,128]{2,1,0:T(1,128)} copy-done((f32[32,1,128]{2,1,0:T(1,128)}, f32[32,1,128]{2,1,0:T(1,128)S(1)}, u32[]{:S(2)}) %copy-start.2) | copy-done | bytes 16408
  17.0 9.5 %second.1 = (f32[1856,128]{1,0:T(8,128)}, f32[8,128]{1,0:T(8,128)}, f32[32,128]{1,0:T(8,128)}) custom-call(s32[1]{0:T(128)} %bitcast.part_ref, s32[1,16]{1,0:T(1,128)} %bitcast.27, s32[1,16]{1,0:T(1,128)} %bitcast.29, f32[1,16]{1,0:T(1,128)} %bitcast.30, s32[2,8]{1,0:T(2,128)} %bitcast.28, f32[3,8,16]{2,1,0:T(8,128)} %grads_ref.1, f32[32,128]{1,0:T(8,128)} %bitcast.24, ...), custom_call_target="tpu_custom_call" | custom-call | flops 1207959552 | bytes 6291456 | tf_op jit(solution)/shard_map/second/pallas_call | solution.py:851
  26.6 0.0 copy-start
  26.6 0.0 copy-start.1
  26.6 17.9 %all_to_all.16 = f32[8,232,128]{2,1,0:T(8,128)S(1)} all-to-all(f32[8,232,128]{2,1,0:T(8,128)} %bitcast.22), channel_id=1, replica_groups=mesh['mesh'=4,'rve'=8] {'rve'}, dimensions={0} | all-to-all | bytes 1900544 | tf_op jit(solution)/shard_map/all_to_all | solution.py:907
  44.5 1.3 %collective-permute-start.1 = (f32[128]{0:T(128)S(1)}, f32[128]{0:T(128)S(1)}, u32[]{:S(2)}, u32[]{:S(2)}) collective-permute-start(f32[128]{0:T(128)S(1)} %slice_reduce_fusion), channel_id=1, source_target_pairs={{8,0},{16,8},{24,16},{9,1},{17,9},{25,17},{10,2},{18,10},{26,18},{... | collective-permute-start | bytes 1544 | tf_op jit(solution)/shard_map/ppermute | solution.py:916
  45.8 4.5 %collective-permute-start = (f32[128]{0:T(128)S(1)}, f32[128]{0:T(128)S(1)}, u32[]{:S(2)}, u32[]{:S(2)}) collective-permute-start(f32[128]{0:T(128)S(1)} %slice_reduce_fusion), channel_id=1, source_target_pairs={{0,8},{8,16},{16,24},{1,9},{9,17},{17,25},{2,10},{10,18},{18,26},{... | collective-permute-start | bytes 1544 | tf_op jit(solution)/shard_map/ppermute | solution.py:915
  50.4 0.0 copy-done
  50.4 0.0 copy-done.1
  50.4 3.0 %third.1 = f32[6,16,4096]{2,1,0:T(8,128)} custom-call(f32[1856,128]{1,0:T(8,128)S(1)} %bitcast.19, f32[2,8,2,8,128]{4,3,2,1,0:T(8,128)S(1)} %copy-done.1, bf16[2,2,2,256,256]{4,3,2,1,0:T(8,128)(2,1)S(1)} %copy-done), custom_call_target="tpu_custom_call" | custom-call | flops 603979776 | bytes 4194304 | tf_op jit(solution)/shard_map/third/pallas_call | solution.py:911
  53.4 0.0 collective-permute-done.1
  53.4 0.0 collective-permute-done
  53.4 0.1 slice_add_fusion
  53.5 0.7 %add.14 = f32[3,4]{1,0:T(4,128)} reshape(f32[12]{0:T(128)S(1)} %slice_add_fusion) | data formatting | bytes 96 | tf_op jit(solution)/shard_map/add | solution.py:919
  (1 shorter events, 0.0 us)
Async XLA Ops:
  2.0 14.4 %all-to-all-start = ((f32[32,1,128]{2,1,0:T(1,128)}), f32[32,1,128]{2,1,0:T(1,128)S(1)}, u32[]{:S(2)}, u32[]{:S(2)}) async-start(f32[32,1,128]{2,1,0:T(1,128)} %bitcast.25), calls=%async_computation | async-start | bytes 32768 | tf_op jit(solution)/shard_map/all_to_all | solution.py:808
  16.4 0.6 %copy-start.2 = (f32[32,1,128]{2,1,0:T(1,128)}, f32[32,1,128]{2,1,0:T(1,128)S(1)}, u32[]{:S(2)}) copy-start(f32[32,1,128]{2,1,0:T(1,128)S(1)} %all-to-all-done) | copy-start | bytes 49156
  26.6 23.8 %copy-start = (bf16[2,2,2,256,256]{4,3,2,1,0:T(8,128)(2,1)S(1)}, bf16[2,2,2,256,256]{4,3,2,1,0:T(8,128)(2,1)}, u32[]{:S(2)}) copy-start(bf16[2,2,2,256,256]{4,3,2,1,0:T(8,128)(2,1)} %constant.14.clone.inverse_hbm) | copy-start | bytes 3145732
  26.6 23.8 %copy-start.1 = (f32[2,8,2,8,128]{4,3,2,1,0:T(8,128)S(1)}, f32[2,8,2,8,128]{4,3,2,1,0:T(8,128)}, u32[]{:S(2)}) copy-start(f32[2,8,2,8,128]{4,3,2,1,0:T(8,128)} %constant.15.clone.normals_ref) | copy-start | bytes 393220
  44.5 8.9 %collective-permute-start.1 = (f32[128]{0:T(128)S(1)}, f32[128]{0:T(128)S(1)}, u32[]{:S(2)}, u32[]{:S(2)}) collective-permute-start(f32[128]{0:T(128)S(1)} %slice_reduce_fusion), channel_id=1, source_target_pairs={{8,0},{16,8},{24,16},{9,1},{17,9},{25,17},{10,2},{18,10},{26,18},{... | collective-permute-start | bytes 1544 | tf_op jit(solution)/shard_map/ppermute | solution.py:916
  45.8 7.6 %collective-permute-start = (f32[128]{0:T(128)S(1)}, f32[128]{0:T(128)S(1)}, u32[]{:S(2)}, u32[]{:S(2)}) collective-permute-start(f32[128]{0:T(128)S(1)} %slice_reduce_fusion), channel_id=1, source_target_pairs={{0,8},{8,16},{16,24},{1,9},{9,17},{17,25},{2,10},{10,18},{18,26},{... | collective-permute-start | bytes 1544 | tf_op jit(solution)/shard_map/ppermute | solution.py:915

commit v2 on v1

--- a/solution.py
+++ b/solution.py
@@ -18,8 +18,6 @@
 LANES = 128
 WINDOW = 32
 SPLIT = 24
-PREV_LANE = 16
-NEXT_LANE = 32
 
 
 def signed_waves(side):
@@ -209,13 +207,14 @@
     return jnp.concatenate([row, jnp.zeros((1, LANES - row.shape[1]), F32)], axis=1)
 
 
-def slot_choice(owner_ref, points, owners, dense):
+def slot_choice(owner_ref, place, points, owners, dense):
     lane = lax.broadcasted_iota(jnp.int32, (points, LANES), 1)
     sub = lax.broadcasted_iota(jnp.int32, (points, LANES), 0)
     diagonal = lane == sub
     if not dense:
         return jnp.where(diagonal, 1.0, 0.0), lane
-    owner_row = padded_row(owner_ref)
+    owner_row = padded_row(owner_ref) - place.astype(F32)
+    owner_row = jnp.where(owner_row < 0, owner_row + float(owners), owner_row)
     owner_col = row_to_column(owner_row, diagonal)
     earlier = jnp.where((owner_col == owner_row) & (lane < sub), 1.0, 0.0)
     rank_col = jnp.sum(earlier, axis=1, keepdims=True)
@@ -277,7 +276,7 @@
 
 
 def first_kernel(
-    dims, owner_ref, warm_hbm, moduli_hbm, forward_hbm,
+    dims, place_ref, owner_ref, warm_hbm, moduli_hbm, forward_hbm,
     spec_hbm, both_hbm, mean_ref,
     forward, warm, moduli, spec, tau, high, low, sems,
 ):
@@ -303,7 +302,7 @@
     for copy in moduli_copies + warm_copies + [table_copy]:
         copy.start()
     octets = points // 8
-    choose, lane = slot_choice(owner_ref, points, owners, dense)
+    choose, lane = slot_choice(owner_ref, place_ref[0], points, owners, dense)
     pick = jnp.sum(choose * lane.astype(F32), axis=1, keepdims=True).astype(jnp.int32)
     picks = [jnp.broadcast_to(pick[8 * o : 8 * o + 8], (8, LANES)) for o in range(octets)]
     locals_ = [
@@ -383,13 +382,17 @@
 
 def second_kernel(
     dims,
-    part_ref, owner_ref, sweeps_ref, weight_ref, conn_ref, grads_ref, table_ref, mean_ref,
+    part_ref, place_ref, owner_ref, sweeps_ref, weight_ref, conn_ref, grads_ref, table_ref, mean_ref,
     normals_ref, first_hbm, both_hbm, forward_hbm, inverse_hbm,
-    send_ref, stress_ref, force_ref,
-    first_ref, both, forward, inverse, tau, high, low, spec, pot, edge, full, macro_buf, loads_buf,
-    sems, slab_sems,
+    *refs,
 ):
     points, comps, side, devices, node_dev, halo, row_span, nodes_part, owners, dense = dims
+    blocks = owners if dense else 1
+    leave_refs, (stress_ref, force_ref) = refs[:blocks], refs[blocks : blocks + 2]
+    (
+        send_ref, first_ref, both, forward, inverse, tau, high, low, spec, pot, edge, full,
+        macro_buf, sems, slab_sems, leave_sems,
+    ) = refs[blocks + 2 :]
     copies = [
         pltpu.make_async_copy(inverse_hbm, inverse, sems.at[0]),
         pltpu.make_async_copy(both_hbm, both, sems.at[1]),
@@ -409,7 +412,7 @@
     tiles = voxels // LANES
     slabs = side // 2
     part = part_ref[0]
-    choose, _ = slot_choice(owner_ref, points, owners, dense)
+    choose, _ = slot_choice(owner_ref, place_ref[0], points, owners, dense)
     count_col = jnp.sum(choose * padded_row(sweeps_ref), axis=1, keepdims=True)
     weight_row = padded_row(weight_ref)
 
@@ -680,27 +683,35 @@
     last_row = edge_base + 3 * window_rows + 7
     for o in range(octets):
         send(o, last_row, jnp.zeros((8, LANES), F32))
-    if dense:
-        loads_buf[...] = jnp.zeros_like(loads_buf)
-        loads_buf[row_span : row_span + devices] = force
-        near = [
-            loads_buf[pl.ds(pl.multiple_of((part + i) * row_span, row_span), row_span), :]
-            for i in range(3)
-        ]
-        send(
-            0, last_row,
-            near[1] + pltpu.roll(near[0], PREV_LANE, 1) + pltpu.roll(near[2], NEXT_LANE, 1),
+    length = send_ref.shape[0] // blocks
+    leave = [
+        pltpu.make_async_copy(
+            send_ref.at[pl.ds(i * length, length)], leave_refs[i], leave_sems.at[i]
         )
+        for i in range(blocks)
+    ]
+    for copy in leave:
+        copy.start()
+    for copy in leave:
+        copy.wait()
 
 
 def third_kernel(
-    dims, recv_ref, normals_ref, inverse_hbm, out_ref, inverse, high, low, spec, sem
+    dims, place_ref, *refs
 ):
-    points, comps, side = dims
+    points, comps, side, blocks = dims
+    arrived = refs[:blocks]
+    normals_ref, inverse_hbm, out_ref, recv_ref, inverse, high, low, spec, sem = refs[blocks:]
     copy = pltpu.make_async_copy(inverse_hbm, inverse, sem)
     copy.start()
     slabs = side // 2
     block = recv_ref.shape[0] // points
+    length = arrived[0].shape[0]
+    for i in range(blocks):
+        source = place_ref[0] - i
+        source = jnp.where(source < 0, source + blocks, source) if blocks > 1 else 0
+        at = pl.multiple_of(source * length, 8) if blocks > 1 else 0
+        recv_ref[pl.ds(at, length)] = arrived[i][...]
     edge_base = 3 * 4 * slabs
     per_row = LANES // WINDOW
     window_rows = 2 * slabs // per_row
@@ -796,7 +807,8 @@
     wide = -(-(nodes_part + 2 * halo) // LANES) * LANES
     vmem = pl.BlockSpec(memory_space=pltpu.VMEM)
     hbm = pl.BlockSpec(memory_space=pltpu.HBM)
-    params = pltpu.CompilerParams(vmem_limit_bytes=63 << 20)
+    smem = pl.BlockSpec(memory_space=pltpu.SMEM)
+    params = pltpu.CompilerParams(vmem_limit_bytes=62 << 20)
 
     packed = pl.pallas_call(
         functools.partial(pack_kernel, (nodes_part, halo)),
@@ -811,6 +823,7 @@
     sweeps_row = sweeps.reshape(1, points)
     weight_row = point_weights.reshape(1, points)
     part = lax.axis_index("mesh").astype(jnp.int32).reshape(1)
+    place = lax.axis_index("rve").astype(jnp.int32).reshape(1)
     warm = warm_strain.transpose(1, 0, 2)
     moduli_rows = (
         moduli.reshape(points, 2, tiles, LANES).transpose(0, 2, 1, 3).reshape(points, -1, LANES)
@@ -827,7 +840,7 @@
             jax.ShapeDtypeStruct((tiles, 2 * points, LANES), F32),
             jax.ShapeDtypeStruct((more, LANES), F32),
         ),
-        in_specs=[vmem, hbm, hbm, hbm],
+        in_specs=[smem, vmem, hbm, hbm, hbm],
         out_specs=(hbm, hbm, vmem),
         scratch_shapes=[
             table_scratch,
@@ -844,20 +857,22 @@
             flops=2 * 3 * 16 * more * plane * plane, transcendentals=0, bytes_accessed=4 << 20
         ),
         name="first",
-    )(owner_row, warm, moduli_rows, forward)
+    )(place, owner_row, warm, moduli_rows, forward)
 
     dims = (points, comps, side, devices, node_dev, halo, owners, nodes_part, owners, dense)
     block = 3 * 4 * slabs + 3 * (2 * slabs * WINDOW // LANES) + 8
-    send, stress, force = pl.pallas_call(
+    blocks = owners if dense else 1
+    *send, stress, force = pl.pallas_call(
         functools.partial(second_kernel, dims),
         out_shape=(
-            jax.ShapeDtypeStruct((points * block, LANES), F32),
+            *(jax.ShapeDtypeStruct((points * block // blocks, LANES), F32),) * blocks,
             jax.ShapeDtypeStruct((8, LANES), F32),
             jax.ShapeDtypeStruct((devices, LANES), F32),
         ),
-        in_specs=[pl.BlockSpec(memory_space=pltpu.SMEM)] + [vmem] * 8 + [hbm] * 4,
-        out_specs=(vmem,) * 3,
+        in_specs=[smem] * 2 + [vmem] * 8 + [hbm] * 4,
+        out_specs=(hbm,) * blocks + (vmem,) * 2,
         scratch_shapes=[
+            pltpu.VMEM((points * block, LANES), F32),
             pltpu.VMEM((2, slabs, more, plane), F32),
             pltpu.VMEM((tiles, 2 * points, LANES), F32),
             table_scratch,
@@ -870,9 +885,9 @@
             pltpu.VMEM((octets, 3, 2 * slabs, 8, LANES), F32),
             pltpu.VMEM((octets, 3, 2, 8, LANES), F32),
             pltpu.VMEM((comps, points, LANES), F32),
-            pltpu.VMEM((devices + 2 * owners, LANES), F32),
             pltpu.SemaphoreType.DMA((3,)),
             pltpu.SemaphoreType.DMA((slabs,)),
+            pltpu.SemaphoreType.DMA((blocks,)),
         ],
         compiler_params=params,
         cost_estimate=pl.CostEstimate(
@@ -880,16 +895,17 @@
         ),
         name="second",
     )(
-        part, owner_row, sweeps_row, weight_row, conn.T, shape_grads, table, mean, normals,
+        part, place, owner_row, sweeps_row, weight_row, conn.T, shape_grads, table, mean, normals,
         spec, both, forward, inverse,
     )
 
     finish = pl.pallas_call(
-        functools.partial(third_kernel, (points, comps, side)),
+        functools.partial(third_kernel, (points, comps, side, blocks)),
         out_shape=jax.ShapeDtypeStruct((comps, points, voxels), F32),
-        in_specs=[vmem, vmem, hbm],
+        in_specs=[smem] + [vmem] * (blocks + 1) + [hbm],
         out_specs=vmem,
         scratch_shapes=[
+            pltpu.VMEM((points * block, LANES), F32),
             table_scratch,
             pltpu.VMEM((2, slabs, rows, plane), BF16),
             pltpu.VMEM((2, slabs, rows, plane), BF16),
@@ -904,23 +920,14 @@
     )
     comps_out = stress[:comps, :points]
     if dense:
-        received = lax.all_to_all(
-            send.reshape(owners, per_owner * block, LANES), "rve",
-            split_axis=0, concat_axis=0, tiled=True,
-        ).reshape(points * block, LANES)
-        micro = finish(received, normals, inverse).transpose(1, 0, 2)
-        found = received.reshape(owners, per_owner * block, LANES)[:, block - 1]
-        found = jnp.sum(found, axis=0)
-        parts = lax.axis_size("mesh")
-        up = lax.ppermute(found, "mesh", [(i, i + 1) for i in range(parts - 1)])
-        down = lax.ppermute(found, "mesh", [(i + 1, i) for i in range(parts - 1)])
-        count = 3 * node_dev
-        nodal = (
-            found[:count] + up[NEXT_LANE : NEXT_LANE + count] + down[PREV_LANE : PREV_LANE + count]
-        ).reshape(3, node_dev)
+        arrived = [send[0]] + [
+            lax.ppermute(send[i], "rve", [(j, (j + i) % owners) for j in range(owners)])
+            for i in range(1, owners)
+        ]
+        micro = finish(place, *arrived, normals, inverse).transpose(1, 0, 2)
     else:
         slots = owners * per_owner
-        final = finish(send, normals, inverse).transpose(1, 0, 2)
+        final = finish(place, send[0], normals, inverse).transpose(1, 0, 2)
         order = jnp.arange(points, dtype=jnp.int32)
         same = owner[:, None] == owner[None, :]
         rank = jnp.sum((same & (order[None, :] < order[:, None])).astype(jnp.int32), axis=1)
@@ -931,8 +938,8 @@
         flags = lax.all_to_all(flags, "rve", split_axis=0, concat_axis=0, tiled=True)
         filled = jnp.nonzero(flags > 0.5, size=points)[0].astype(jnp.int32)
         micro = fields[filled]
-        pieces = lax.all_to_all(force, axes, split_axis=0, concat_axis=0, tiled=True)
-        nodal = jnp.sum(pieces, axis=0)[: 3 * node_dev].reshape(3, node_dev)
+    pieces = lax.all_to_all(force, axes, split_axis=0, concat_axis=0, tiled=True)
+    nodal = jnp.sum(pieces, axis=0)[: 3 * node_dev].reshape(3, node_dev)
     return (nodal, comps_out, micro)
 
 

time: 54.4 us -> 53.3 us (0.980)
  blocking collectives: 17.9 us -> 11.6 us
  waiting for transfers between devices: 0.56 us -> 2.84 us
  starting transfers between devices: 13.2 us -> 14.5 us
  local copies, waits for them, and re-layouts: 1.28 us -> 2.16 us
  Pallas kernels: 20.4 us -> 21.1 us
    all_to_all x1, blocking collectives: 17.9 us -> 11.6 us  [on_device(): lax.all_to_all(force, axes, split_axis=0, concat_axis=0, tiled=True)]
    ppermute x2 -> x7, waiting for transfers between devices: 0.01 us -> 2.2 us  [on_device(): lax.ppermute(send[i], 'rve', [(j, (j + i) % owners) for j in range(owners)])]
    ppermute x2 -> x7, starting transfers between devices: 5.83 us -> 7.21 us  [on_device(): lax.ppermute(send[i], 'rve', [(j, (j + i) % owners) for j in range(owners)])]
    unnamed x6 -> x8, local copies, waits for them, and re-layouts: 0.61 us -> 1.5 us
    pallas_call x2, Pallas kernels: 12.5 us -> 13.2 us  [the longest x1 10.2 us: on_device(): pl.pallas_call(functools.partial(second_kernel, dims), out_shape=(*(jax.S...]
    add x1 -> x0, local copies, waits for them, and re-layouts: 0.66 us -> none  [on_device(): found[:count] + up[NEXT_LANE:NEXT_LANE + count]]
    reshape x0 -> x1, local copies, waits for them, and re-layouts: none -> 0.66 us  [on_device(): nodal = jnp.sum(pieces, axis=0)[:3 * node_dev].reshape(3, node_dev)]
  transfers between devices with their start and end apart: 3 -> 8, of which waited for: 1 -> 3; matrix products, arithmetic and copies ran while one was open for 0% -> 1% of each run, Pallas kernels for 18% -> 12%
where the time goes in v2:
time: 53.3 us; the launch traced here: 53 us
  Pallas kernels  21.1 us (40%)
  starting transfers between devices  14.5 us (27%)
  blocking collectives  11.6 us (22%)
  waiting for transfers between devices  2.84 us (5%)
  local copies, waits for them, and re-layouts  2.16 us (4%)
  between operations  0.72 us (1%)
    all_to_all x1, blocking collectives, on_device(): lax.all_to_all(force, axes, split_axis=0, concat_axis=0, tiled=True)  11.6 us
    pallas_call x1, Pallas kernels, on_device(): pl.pallas_call(functools.partial(second_kernel, dims), out_shape=(*(jax.S...  10.2 us
    all_to_all x1, starting transfers between devices, on_device(): lax.all_to_all(packed, axes, split_axis=0, concat_axis=0, tiled=True)  7.33 us
    ppermute x7, starting transfers between devices, on_device(): lax.ppermute(send[i], 'rve', [(j, (j + i) % owners) for j in range(owners)])  7.21 us
    pallas_call x1, Pallas kernels, on_device(): pl.pallas_call(functools.partial(first_kernel, (points, comps, side, owne...  6.52 us
    pallas_call x1, Pallas kernels, on_device(): micro = finish(place, *arrived, normals, inverse).transpose(1, 0, 2)  3.05 us
    ppermute x7, waiting for transfers between devices, on_device(): lax.ppermute(send[i], 'rve', [(j, (j + i) % owners) for j in range(owners)])  2.2 us
    unnamed x8, local copies, waits for them, and re-layouts  1.5 us
  transfers between devices with their start and end apart: 8, of which 3 were waited for; matrix products, arithmetic and copies ran while one was open for 1% of the time, Pallas kernels for 12%

profile of v2, /device:TPU:0, one launch (start us, length us, event | category | flops | bytes accessed | tf_op | source)
XLA Modules:
  0.0 53.0 jit_solution(3168928764270191448)
XLA Ops:
  0.6 1.4 %pack.1 = f32[32,128]{1,0:T(8,128)} custom-call(f32[3,4]{1,0:T(4,128)} %displacement_ref.1, s32[2,8]{1,0:T(2,128)} %halo_ref.1), custom_call_target="tpu_custom_call" | custom-call | tf_op jit(solution)/shard_map/pack/pallas_call | solution.py:813
  2.0 7.3 %all-to-all-start = ((f32[32,1,128]{2,1,0:T(1,128)}), f32[32,1,128]{2,1,0:T(1,128)S(1)}, u32[]{:S(2)}, u32[]{:S(2)}) async-start(f32[32,1,128]{2,1,0:T(1,128)} %bitcast.26), calls=%async_computation | async-start | bytes 32768 | tf_op jit(solution)/shard_map/all_to_all | solution.py:820
  9.3 6.5 %first.1 = (f32[2,8,128,256]{3,2,1,0:T(8,128)}, f32[32,32,128]{2,1,0:T(8,128)}, f32[128,128]{1,0:T(8,128)}) custom-call(s32[1]{0:T(128)} %bitcast.1.place_ref, s32[1,16]{1,0:T(1,128)} %bitcast.28, f32[6,16,4096]{2,1,0:T(8,128)} %bitcast.22, f32[16,64,128]{2,1,0:T(8,128)} %bitcast.24, bf16[2,2,2,256,256]{4,3,2,1,0:T(8,128)(2,1)} %constant.16.clone.forward_hbm), custom_call_target="tpu_custom_call" | custom-call | flops 805306368 | bytes 4194304 | tf_op jit(solution)/shard_map/first/pallas_call | solution.py:836
  15.9 0.6 %all-to-all-done = f32[32,1,128]{2,1,0:T(1,128)S(1)} async-done(((f32[32,1,128]{2,1,0:T(1,128)}), f32[32,1,128]{2,1,0:T(1,128)S(1)}, u32[]{:S(2)}, u32[]{:S(2)}) %all-to-all-start) | async-done | bytes 16416 | tf_op jit(solution)/shard_map/all_to_all | solution.py:820
  16.5 0.6 %copy-done.3 = f32[32,1,128]{2,1,0:T(1,128)} copy-done((f32[32,1,128]{2,1,0:T(1,128)}, f32[32,1,128]{2,1,0:T(1,128)S(1)}, u32[]{:S(2)}) %copy-start.3) | copy-done | bytes 16408
  17.1 10.2 %second.1 = (f32[232,128]{1,0:T(8,128)}, f32[232,128]{1,0:T(8,128)}, f32[232,128]{1,0:T(8,128)}, f32[232,128]{1,0:T(8,128)}, f32[232,128]{1,0:T(8,128)}, /*index...) custom-call(s32[1]{0:T(128)} %bitcast.part_ref, ...), custom_call_target="tpu_custom_call" | custom-call | flops 1207959552 | bytes 6291456 | tf_op jit(solution)/shard_map/second/pallas_call | solution.py:865
  27.3 0.1 collective-permute-start
  27.4 1.3 %collective-permute-start.1 = (f32[232,128]{1,0:T(8,128)}, f32[232,128]{1,0:T(8,128)S(1)}, u32[]{:S(2)}, u32[]{:S(2)}) collective-permute-start(f32[232,128]{1,0:T(8,128)} %get-tuple-element.23), channel_id=1, source_target_pairs={{0,2},{1,3},{2,4},{3,5},{4,6},{5,7},{6,0},{7,1},{8,10},{9,11},{10,... | collective-permute-start | bytes 356360 | tf_op jit(solution)/shard_map/ppermute | solution.py:924
  28.6 2.2 %collective-permute-start.2 = (f32[232,128]{1,0:T(8,128)}, f32[232,128]{1,0:T(8,128)S(1)}, u32[]{:S(2)}, u32[]{:S(2)}) collective-permute-start(f32[232,128]{1,0:T(8,128)} %get-tuple-element.24), channel_id=1, source_target_pairs={{0,3},{1,4},{2,5},{3,6},{4,7},{5,0},{6,1},{7,2},{8,11},{9,12},{10,... | collective-permute-start | bytes 356360 | tf_op jit(solution)/shard_map/ppermute | solution.py:924
  30.9 0.6 %collective-permute-start.3 = (f32[232,128]{1,0:T(8,128)}, f32[232,128]{1,0:T(8,128)S(1)}, u32[]{:S(2)}, u32[]{:S(2)}) collective-permute-start(f32[232,128]{1,0:T(8,128)} %get-tuple-element.25), channel_id=1, source_target_pairs={{0,4},{1,5},{2,6},{3,7},{4,0},{5,1},{6,2},{7,3},{8,12},{9,13},{10,... | collective-permute-start | bytes 356360 | tf_op jit(solution)/shard_map/ppermute | solution.py:924
  31.4 0.1 collective-permute-start.4
  31.5 1.9 %collective-permute-done.refs_1_ = f32[232,128]{1,0:T(8,128)S(1)} collective-permute-done((f32[232,128]{1,0:T(8,128)}, f32[232,128]{1,0:T(8,128)S(1)}, u32[]{:S(2)}, u32[]{:S(2)}) %collective-permute-start) | collective-permute-done | bytes 118816 | tf_op jit(solution)/shard_map/ppermute | solution.py:924
  33.4 1.0 %collective-permute-start.5 = (f32[232,128]{1,0:T(8,128)}, f32[232,128]{1,0:T(8,128)S(1)}, u32[]{:S(2)}, u32[]{:S(2)}) collective-permute-start(f32[232,128]{1,0:T(8,128)} %get-tuple-element.27), channel_id=1, source_target_pairs={{0,6},{1,7},{2,0},{3,1},{4,2},{5,3},{6,4},{7,5},{8,14},{9,15},{10,... | collective-permute-start | bytes 356360 | tf_op jit(solution)/shard_map/ppermute | solution.py:924
  34.4 0.3 collective-permute-done.1.refs_2_
  34.7 2.0 %collective-permute-start.6 = (f32[232,128]{1,0:T(8,128)}, f32[232,128]{1,0:T(8,128)S(1)}, u32[]{:S(2)}, u32[]{:S(2)}) collective-permute-start(f32[232,128]{1,0:T(8,128)} %get-tuple-element.28), channel_id=1, source_target_pairs={{0,7},{1,0},{2,1},{3,2},{4,3},{5,4},{6,5},{7,6},{8,15},{9,8},{10,9... | collective-permute-start | bytes 356360 | tf_op jit(solution)/shard_map/ppermute | solution.py:924
  36.7 11.6 %all_to_all.20 = f32[32,1,128]{2,1,0:T(1,128)S(1)} all-to-all(f32[32,1,128]{2,1,0:T(1,128)} %bitcast.27), channel_id=1, replica_groups=mesh['mesh'=4,'rve'=8] {'mesh','rve'}, dimensions={0} | all-to-all | bytes 32768 | tf_op jit(solution)/shard_map/all_to_all | solution.py:941
  48.3 0.1 reduce_sum.9
  48.4 0.7 %reshape.49 = f32[3,4]{1,0:T(4,128)} reshape(f32[12]{0:T(128)S(1)} %bitcast.30) | data formatting | bytes 96 | tf_op jit(solution)/shard_map/reshape | solution.py:942
  49.0 0.0 collective-permute-done.2.refs_3_
  49.0 0.0 collective-permute-done.3.refs_4_
  49.0 0.0 collective-permute-done.4.refs_5_
  49.0 0.0 collective-permute-done.5.refs_6_
  49.1 0.9 %copy-done.2 = f32[232,128]{1,0:T(8,128)S(1)} copy-done((f32[232,128]{1,0:T(8,128)S(1)}, f32[232,128]{1,0:T(8,128)}, u32[]{:S(2)}) %copy-start.2) | copy-done | bytes 118808
  50.0 3.0 %third.1 = f32[6,16,4096]{2,1,0:T(8,128)} custom-call(s32[1]{0:T(128)} %bitcast.1.place_ref, f32[232,128]{1,0:T(8,128)S(1)} %copy-done.2, f32[232,128]{1,0:T(8,128)S(1)} %collective-permute-done.refs_1_, f32[232,128]{1,0:T(8,128)S(1)} %collective-permute-done.1.refs_2_, f32[232,128]{1,0:T(8,128)S(1)} %collective-permute-done.2.refs_3_, ...), custom_call_target="tpu_custom_call" | custom-call | flops 603979776 | bytes 4194304 | tf_op jit(solution)/shard_map/third/pallas_call | solution.py:927
  (7 shorter events, 0.0 us)
Async XLA Ops:
  2.0 14.5 %all-to-all-start = ((f32[32,1,128]{2,1,0:T(1,128)}), f32[32,1,128]{2,1,0:T(1,128)S(1)}, u32[]{:S(2)}, u32[]{:S(2)}) async-start(f32[32,1,128]{2,1,0:T(1,128)} %bitcast.26), calls=%async_computation | async-start | bytes 32768 | tf_op jit(solution)/shard_map/all_to_all | solution.py:820
  16.5 0.6 %copy-start.3 = (f32[32,1,128]{2,1,0:T(1,128)}, f32[32,1,128]{2,1,0:T(1,128)S(1)}, u32[]{:S(2)}) copy-start(f32[32,1,128]{2,1,0:T(1,128)S(1)} %all-to-all-done) | copy-start | bytes 49156
  17.1 31.9 %copy-start = (bf16[2,2,2,256,256]{4,3,2,1,0:T(8,128)(2,1)S(1)}, bf16[2,2,2,256,256]{4,3,2,1,0:T(8,128)(2,1)}, u32[]{:S(2)}) copy-start(bf16[2,2,2,256,256]{4,3,2,1,0:T(8,128)(2,1)} %constant.17.clone.inverse_hbm.refs_9_) | copy-start | bytes 3145732
  17.1 32.0 %copy-start.1 = (f32[2,8,2,8,128]{4,3,2,1,0:T(8,128)S(1)}, f32[2,8,2,8,128]{4,3,2,1,0:T(8,128)}, u32[]{:S(2)}) copy-start(f32[2,8,2,8,128]{4,3,2,1,0:T(8,128)} %constant.18.clone.normals_ref.refs_8_) | copy-start | bytes 393220
  27.3 6.2 %collective-permute-start = (f32[232,128]{1,0:T(8,128)}, f32[232,128]{1,0:T(8,128)S(1)}, u32[]{:S(2)}, u32[]{:S(2)}) collective-permute-start(f32[232,128]{1,0:T(8,128)} %get-tuple-element.22), channel_id=1, source_target_pairs={{0,1},{1,2},{2,3},{3,4},{4,5},{5,6},{6,7},{7,0},{8,9},{9,10},{10,1... | collective-permute-start | bytes 356360 | tf_op jit(solution)/shard_map/ppermute | solution.py:924
  27.4 7.4 %collective-permute-start.1 = (f32[232,128]{1,0:T(8,128)}, f32[232,128]{1,0:T(8,128)S(1)}, u32[]{:S(2)}, u32[]{:S(2)}) collective-permute-start(f32[232,128]{1,0:T(8,128)} %get-tuple-element.23), channel_id=1, source_target_pairs={{0,2},{1,3},{2,4},{3,5},{4,6},{5,7},{6,0},{7,1},{8,10},{9,11},{10,... | collective-permute-start | bytes 356360 | tf_op jit(solution)/shard_map/ppermute | solution.py:924
  28.6 20.4 %collective-permute-start.2 = (f32[232,128]{1,0:T(8,128)}, f32[232,128]{1,0:T(8,128)S(1)}, u32[]{:S(2)}, u32[]{:S(2)}) collective-permute-start(f32[232,128]{1,0:T(8,128)} %get-tuple-element.24), channel_id=1, source_target_pairs={{0,3},{1,4},{2,5},{3,6},{4,7},{5,0},{6,1},{7,2},{8,11},{9,12},{10,... | collective-permute-start | bytes 356360 | tf_op jit(solution)/shard_map/ppermute | solution.py:924
  30.9 18.2 %collective-permute-start.3 = (f32[232,128]{1,0:T(8,128)}, f32[232,128]{1,0:T(8,128)S(1)}, u32[]{:S(2)}, u32[]{:S(2)}) collective-permute-start(f32[232,128]{1,0:T(8,128)} %get-tuple-element.25), channel_id=1, source_target_pairs={{0,4},{1,5},{2,6},{3,7},{4,0},{5,1},{6,2},{7,3},{8,12},{9,13},{10,... | collective-permute-start | bytes 356360 | tf_op jit(solution)/shard_map/ppermute | solution.py:924
  31.4 17.6 %collective-permute-start.4 = (f32[232,128]{1,0:T(8,128)}, f32[232,128]{1,0:T(8,128)S(1)}, u32[]{:S(2)}, u32[]{:S(2)}) collective-permute-start(f32[232,128]{1,0:T(8,128)} %get-tuple-element.26), channel_id=1, source_target_pairs={{0,5},{1,6},{2,7},{3,0},{4,1},{5,2},{6,3},{7,4},{8,13},{9,14},{10,... | collective-permute-start | bytes 356360 | tf_op jit(solution)/shard_map/ppermute | solution.py:924
  33.4 15.6 %collective-permute-start.5 = (f32[232,128]{1,0:T(8,128)}, f32[232,128]{1,0:T(8,128)S(1)}, u32[]{:S(2)}, u32[]{:S(2)}) collective-permute-start(f32[232,128]{1,0:T(8,128)} %get-tuple-element.27), channel_id=1, source_target_pairs={{0,6},{1,7},{2,0},{3,1},{4,2},{5,3},{6,4},{7,5},{8,14},{9,15},{10,... | collective-permute-start | bytes 356360 | tf_op jit(solution)/shard_map/ppermute | solution.py:924
  34.7 14.3 %collective-permute-start.6 = (f32[232,128]{1,0:T(8,128)}, f32[232,128]{1,0:T(8,128)S(1)}, u32[]{:S(2)}, u32[]{:S(2)}) collective-permute-start(f32[232,128]{1,0:T(8,128)} %get-tuple-element.28), channel_id=1, source_target_pairs={{0,7},{1,0},{2,1},{3,2},{4,3},{5,4},{6,5},{7,6},{8,15},{9,8},{10,9... | collective-permute-start | bytes 356360 | tf_op jit(solution)/shard_map/ppermute | solution.py:924
  49.1 0.9 %copy-start.2 = (f32[232,128]{1,0:T(8,128)S(1)}, f32[232,128]{1,0:T(8,128)}, u32[]{:S(2)}) copy-start(f32[232,128]{1,0:T(8,128)} %get-tuple-element.21.refs_0_) | copy-start | bytes 356356

commit v3 on v2

--- a/solution.py
+++ b/solution.py
@@ -391,7 +391,7 @@
     leave_refs, (stress_ref, force_ref) = refs[:blocks], refs[blocks : blocks + 2]
     (
         send_ref, first_ref, both, forward, inverse, tau, high, low, spec, pot, edge, full,
-        macro_buf, sems, slab_sems, leave_sems,
+        macro_buf, sems, slab_sems,
     ) = refs[blocks + 2 :]
     copies = [
         pltpu.make_async_copy(inverse_hbm, inverse, sems.at[0]),
@@ -406,8 +406,6 @@
 
     for s in range(side // 2):
         slab_copy(s).start()
-    for copy in copies:
-        copy.start()
     voxels = side**3
     tiles = voxels // LANES
     slabs = side // 2
@@ -588,7 +586,10 @@
         zero = jnp.zeros((8, LANES), F32)
         return lax.fori_loop(0, slabs, step, (zero,) * (octets * (comps + 1)))
 
+    copies[0].start()
     first = green_stage(False)
+    for copy in copies[1:]:
+        copy.start()
     copies[0].wait()
     multiply(high, low, inverse, spec)
 
@@ -638,6 +639,10 @@
         for c in range(comps):
             value = jnp.where(row_lane == c, macro[c][8 * o : 8 * o + 8], value)
         send(o, edge_base + 3 * window_rows + 6, value)
+        send(o, edge_base + 3 * window_rows + 7, jnp.zeros((8, LANES), F32))
+    length = send_ref.shape[0] // blocks
+    for i in range(blocks):
+        leave_refs[i][...] = send_ref[i * length : (i + 1) * length]
 
     sums = []
     for q in range(comps + 1):
@@ -680,20 +685,6 @@
         precision=lax.Precision.HIGHEST,
     )
     force_ref[...] = force
-    last_row = edge_base + 3 * window_rows + 7
-    for o in range(octets):
-        send(o, last_row, jnp.zeros((8, LANES), F32))
-    length = send_ref.shape[0] // blocks
-    leave = [
-        pltpu.make_async_copy(
-            send_ref.at[pl.ds(i * length, length)], leave_refs[i], leave_sems.at[i]
-        )
-        for i in range(blocks)
-    ]
-    for copy in leave:
-        copy.start()
-    for copy in leave:
-        copy.wait()
 
 
 def third_kernel(
@@ -870,7 +861,7 @@
             jax.ShapeDtypeStruct((devices, LANES), F32),
         ),
         in_specs=[smem] * 2 + [vmem] * 8 + [hbm] * 4,
-        out_specs=(hbm,) * blocks + (vmem,) * 2,
+        out_specs=(vmem,) * (blocks + 2),
         scratch_shapes=[
             pltpu.VMEM((points * block, LANES), F32),
             pltpu.VMEM((2, slabs, more, plane), F32),
@@ -887,7 +878,6 @@
             pltpu.VMEM((comps, points, LANES), F32),
             pltpu.SemaphoreType.DMA((3,)),
             pltpu.SemaphoreType.DMA((slabs,)),
-            pltpu.SemaphoreType.DMA((blocks,)),
         ],
         compiler_params=params,
         cost_estimate=pl.CostEstimate(

time: 53.3 us -> 52.7 us (0.989)
  Pallas kernels: 21.1 us -> 20.4 us
    pallas_call x1, Pallas kernels: 10.2 us -> 9.47 us  [on_device(): pl.pallas_call(functools.partial(second_kernel, dims), out_shape=(*(jax.S...]
where the time goes in v3:
time: 52.7 us; the launch traced here: 52.3 us
  Pallas kernels  20.4 us (39%)
  starting transfers between devices  14.6 us (28%)
  blocking collectives  11.6 us (22%)
  waiting for transfers between devices  2.81 us (5%)
  local copies, waits for them, and re-layouts  2.16 us (4%)
  between operations  0.72 us (1%)
    all_to_all x1, blocking collectives, on_device(): lax.all_to_all(force, axes, split_axis=0, concat_axis=0, tiled=True)  11.6 us
    pallas_call x1, Pallas kernels, on_device(): pl.pallas_call(functools.partial(second_kernel, dims), out_shape=(*(jax.S...  9.47 us
    all_to_all x1, starting transfers between devices, on_device(): lax.all_to_all(packed, axes, split_axis=0, concat_axis=0, tiled=True)  7.33 us
    ppermute x7, starting transfers between devices, on_device(): lax.ppermute(send[i], 'rve', [(j, (j + i) % owners) for j in range(owners)])  7.29 us
    pallas_call x1, Pallas kernels, on_device(): pl.pallas_call(functools.partial(first_kernel, (points, comps, side, owne...  6.52 us
    pallas_call x1, Pallas kernels, on_device(): micro = finish(place, *arrived, normals, inverse).transpose(1, 0, 2)  3.05 us
    ppermute x7, waiting for transfers between devices, on_device(): lax.ppermute(send[i], 'rve', [(j, (j + i) % owners) for j in range(owners)])  2.17 us
    unnamed x8, local copies, waits for them, and re-layouts  1.5 us
  transfers between devices with their start and end apart: 8, of which 3 were waited for; matrix products, arithmetic and copies ran while one was open for 1% of the time, Pallas kernels for 12%

profile of v3, /device:TPU:0, one launch (start us, length us, event | category | flops | bytes accessed | tf_op | source)
XLA Modules:
  0.0 52.3 jit_solution(14903703481926062811)
XLA Ops:
  0.6 1.4 %pack.1 = f32[32,128]{1,0:T(8,128)} custom-call(f32[3,4]{1,0:T(4,128)} %displacement_ref.1, s32[2,8]{1,0:T(2,128)} %halo_ref.1), custom_call_target="tpu_custom_call" | custom-call | tf_op jit(solution)/shard_map/pack/pallas_call | solution.py:804
  2.0 7.3 %all-to-all-start = ((f32[32,1,128]{2,1,0:T(1,128)}), f32[32,1,128]{2,1,0:T(1,128)S(1)}, u32[]{:S(2)}, u32[]{:S(2)}) async-start(f32[32,1,128]{2,1,0:T(1,128)} %bitcast.26), calls=%async_computation | async-start | bytes 32768 | tf_op jit(solution)/shard_map/all_to_all | solution.py:811
  9.3 6.5 %first.1 = (f32[2,8,128,256]{3,2,1,0:T(8,128)}, f32[32,32,128]{2,1,0:T(8,128)}, f32[128,128]{1,0:T(8,128)}) custom-call(s32[1]{0:T(128)} %bitcast.1.place_ref, s32[1,16]{1,0:T(1,128)} %bitcast.28, f32[6,16,4096]{2,1,0:T(8,128)} %bitcast.22, f32[16,64,128]{2,1,0:T(8,128)} %bitcast.24, bf16[2,2,2,256,256]{4,3,2,1,0:T(8,128)(2,1)} %constant.16.clone.forward_hbm), custom_call_target="tpu_custom_call" | custom-call | flops 805306368 | bytes 4194304 | tf_op jit(solution)/shard_map/first/pallas_call | solution.py:827
  15.9 0.6 %all-to-all-done = f32[32,1,128]{2,1,0:T(1,128)S(1)} async-done(((f32[32,1,128]{2,1,0:T(1,128)}), f32[32,1,128]{2,1,0:T(1,128)S(1)}, u32[]{:S(2)}, u32[]{:S(2)}) %all-to-all-start) | async-done | bytes 16416 | tf_op jit(solution)/shard_map/all_to_all | solution.py:811
  16.5 0.6 %copy-done.3 = f32[32,1,128]{2,1,0:T(1,128)} copy-done((f32[32,1,128]{2,1,0:T(1,128)}, f32[32,1,128]{2,1,0:T(1,128)S(1)}, u32[]{:S(2)}) %copy-start.3) | copy-done | bytes 16408
  17.1 9.5 %second.1 = (f32[232,128]{1,0:T(8,128)}, f32[232,128]{1,0:T(8,128)}, f32[232,128]{1,0:T(8,128)}, f32[232,128]{1,0:T(8,128)}, f32[232,128]{1,0:T(8,128)}, /*index...) custom-call(s32[1]{0:T(128)} %bitcast.part_ref, ...), custom_call_target="tpu_custom_call" | custom-call | flops 1207959552 | bytes 6291456 | tf_op jit(solution)/shard_map/second/pallas_call | solution.py:856
  26.6 0.1 collective-permute-start
  26.7 1.3 %collective-permute-start.1 = (f32[232,128]{1,0:T(8,128)}, f32[232,128]{1,0:T(8,128)S(1)}, u32[]{:S(2)}, u32[]{:S(2)}) collective-permute-start(f32[232,128]{1,0:T(8,128)} %get-tuple-element.23), channel_id=1, source_target_pairs={{0,2},{1,3},{2,4},{3,5},{4,6},{5,7},{6,0},{7,1},{8,10},{9,11},{10,... | collective-permute-start | bytes 356360 | tf_op jit(solution)/shard_map/ppermute | solution.py:914
  27.9 2.2 %collective-permute-start.2 = (f32[232,128]{1,0:T(8,128)}, f32[232,128]{1,0:T(8,128)S(1)}, u32[]{:S(2)}, u32[]{:S(2)}) collective-permute-start(f32[232,128]{1,0:T(8,128)} %get-tuple-element.24), channel_id=1, source_target_pairs={{0,3},{1,4},{2,5},{3,6},{4,7},{5,0},{6,1},{7,2},{8,11},{9,12},{10,... | collective-permute-start | bytes 356360 | tf_op jit(solution)/shard_map/ppermute | solution.py:914
  30.2 0.6 %collective-permute-start.3 = (f32[232,128]{1,0:T(8,128)}, f32[232,128]{1,0:T(8,128)S(1)}, u32[]{:S(2)}, u32[]{:S(2)}) collective-permute-start(f32[232,128]{1,0:T(8,128)} %get-tuple-element.25), channel_id=1, source_target_pairs={{0,4},{1,5},{2,6},{3,7},{4,0},{5,1},{6,2},{7,3},{8,12},{9,13},{10,... | collective-permute-start | bytes 356360 | tf_op jit(solution)/shard_map/ppermute | solution.py:914
  30.7 0.1 collective-permute-start.4
  30.8 1.9 %collective-permute-done.refs_1_ = f32[232,128]{1,0:T(8,128)S(1)} collective-permute-done((f32[232,128]{1,0:T(8,128)}, f32[232,128]{1,0:T(8,128)S(1)}, u32[]{:S(2)}, u32[]{:S(2)}) %collective-permute-start) | collective-permute-done | bytes 118816 | tf_op jit(solution)/shard_map/ppermute | solution.py:914
  32.7 1.0 %collective-permute-start.5 = (f32[232,128]{1,0:T(8,128)}, f32[232,128]{1,0:T(8,128)S(1)}, u32[]{:S(2)}, u32[]{:S(2)}) collective-permute-start(f32[232,128]{1,0:T(8,128)} %get-tuple-element.27), channel_id=1, source_target_pairs={{0,6},{1,7},{2,0},{3,1},{4,2},{5,3},{6,4},{7,5},{8,14},{9,15},{10,... | collective-permute-start | bytes 356360 | tf_op jit(solution)/shard_map/ppermute | solution.py:914
  33.8 0.2 collective-permute-done.1.refs_2_
  34.0 2.0 %collective-permute-start.6 = (f32[232,128]{1,0:T(8,128)}, f32[232,128]{1,0:T(8,128)S(1)}, u32[]{:S(2)}, u32[]{:S(2)}) collective-permute-start(f32[232,128]{1,0:T(8,128)} %get-tuple-element.28), channel_id=1, source_target_pairs={{0,7},{1,0},{2,1},{3,2},{4,3},{5,4},{6,5},{7,6},{8,15},{9,8},{10,9... | collective-permute-start | bytes 356360 | tf_op jit(solution)/shard_map/ppermute | solution.py:914
  36.0 11.6 %all_to_all.20 = f32[32,1,128]{2,1,0:T(1,128)S(1)} all-to-all(f32[32,1,128]{2,1,0:T(1,128)} %bitcast.27), channel_id=1, replica_groups=mesh['mesh'=4,'rve'=8] {'mesh','rve'}, dimensions={0} | all-to-all | bytes 32768 | tf_op jit(solution)/shard_map/all_to_all | solution.py:931
  47.6 0.1 reduce_sum.9
  47.7 0.7 %reshape.49 = f32[3,4]{1,0:T(4,128)} reshape(f32[12]{0:T(128)S(1)} %bitcast.30) | data formatting | bytes 96 | tf_op jit(solution)/shard_map/reshape | solution.py:932
  48.3 0.0 collective-permute-done.2.refs_3_
  48.3 0.0 collective-permute-done.3.refs_4_
  48.3 0.0 collective-permute-done.4.refs_5_
  48.3 0.0 collective-permute-done.5.refs_6_
  48.4 0.9 %copy-done.2 = f32[232,128]{1,0:T(8,128)S(1)} copy-done((f32[232,128]{1,0:T(8,128)S(1)}, f32[232,128]{1,0:T(8,128)}, u32[]{:S(2)}) %copy-start.2) | copy-done | bytes 118808
  49.3 3.1 %third.1 = f32[6,16,4096]{2,1,0:T(8,128)} custom-call(s32[1]{0:T(128)} %bitcast.1.place_ref, f32[232,128]{1,0:T(8,128)S(1)} %copy-done.2, f32[232,128]{1,0:T(8,128)S(1)} %collective-permute-done.refs_1_, f32[232,128]{1,0:T(8,128)S(1)} %collective-permute-done.1.refs_2_, f32[232,128]{1,0:T(8,128)S(1)} %collective-permute-done.2.refs_3_, ...), custom_call_target="tpu_custom_call" | custom-call | flops 603979776 | bytes 4194304 | tf_op jit(solution)/shard_map/third/pallas_call | solution.py:917
  (7 shorter events, 0.0 us)
Async XLA Ops:
  2.0 14.5 %all-to-all-start = ((f32[32,1,128]{2,1,0:T(1,128)}), f32[32,1,128]{2,1,0:T(1,128)S(1)}, u32[]{:S(2)}, u32[]{:S(2)}) async-start(f32[32,1,128]{2,1,0:T(1,128)} %bitcast.26), calls=%async_computation | async-start | bytes 32768 | tf_op jit(solution)/shard_map/all_to_all | solution.py:811
  16.5 0.6 %copy-start.3 = (f32[32,1,128]{2,1,0:T(1,128)}, f32[32,1,128]{2,1,0:T(1,128)S(1)}, u32[]{:S(2)}) copy-start(f32[32,1,128]{2,1,0:T(1,128)S(1)} %all-to-all-done) | copy-start | bytes 49156
  17.1 31.2 %copy-start = (bf16[2,2,2,256,256]{4,3,2,1,0:T(8,128)(2,1)S(1)}, bf16[2,2,2,256,256]{4,3,2,1,0:T(8,128)(2,1)}, u32[]{:S(2)}) copy-start(bf16[2,2,2,256,256]{4,3,2,1,0:T(8,128)(2,1)} %constant.17.clone.inverse_hbm.refs_9_) | copy-start | bytes 3145732
  17.1 31.3 %copy-start.1 = (f32[2,8,2,8,128]{4,3,2,1,0:T(8,128)S(1)}, f32[2,8,2,8,128]{4,3,2,1,0:T(8,128)}, u32[]{:S(2)}) copy-start(f32[2,8,2,8,128]{4,3,2,1,0:T(8,128)} %constant.18.clone.normals_ref.refs_8_) | copy-start | bytes 393220
  26.6 6.2 %collective-permute-start = (f32[232,128]{1,0:T(8,128)}, f32[232,128]{1,0:T(8,128)S(1)}, u32[]{:S(2)}, u32[]{:S(2)}) collective-permute-start(f32[232,128]{1,0:T(8,128)} %get-tuple-element.22), channel_id=1, source_target_pairs={{0,1},{1,2},{2,3},{3,4},{4,5},{5,6},{6,7},{7,0},{8,9},{9,10},{10,1... | collective-permute-start | bytes 356360 | tf_op jit(solution)/shard_map/ppermute | solution.py:914
  26.7 7.4 %collective-permute-start.1 = (f32[232,128]{1,0:T(8,128)}, f32[232,128]{1,0:T(8,128)S(1)}, u32[]{:S(2)}, u32[]{:S(2)}) collective-permute-start(f32[232,128]{1,0:T(8,128)} %get-tuple-element.23), channel_id=1, source_target_pairs={{0,2},{1,3},{2,4},{3,5},{4,6},{5,7},{6,0},{7,1},{8,10},{9,11},{10,... | collective-permute-start | bytes 356360 | tf_op jit(solution)/shard_map/ppermute | solution.py:914
  27.9 20.4 %collective-permute-start.2 = (f32[232,128]{1,0:T(8,128)}, f32[232,128]{1,0:T(8,128)S(1)}, u32[]{:S(2)}, u32[]{:S(2)}) collective-permute-start(f32[232,128]{1,0:T(8,128)} %get-tuple-element.24), channel_id=1, source_target_pairs={{0,3},{1,4},{2,5},{3,6},{4,7},{5,0},{6,1},{7,2},{8,11},{9,12},{10,... | collective-permute-start | bytes 356360 | tf_op jit(solution)/shard_map/ppermute | solution.py:914
  30.2 18.2 %collective-permute-start.3 = (f32[232,128]{1,0:T(8,128)}, f32[232,128]{1,0:T(8,128)S(1)}, u32[]{:S(2)}, u32[]{:S(2)}) collective-permute-start(f32[232,128]{1,0:T(8,128)} %get-tuple-element.25), channel_id=1, source_target_pairs={{0,4},{1,5},{2,6},{3,7},{4,0},{5,1},{6,2},{7,3},{8,12},{9,13},{10,... | collective-permute-start | bytes 356360 | tf_op jit(solution)/shard_map/ppermute | solution.py:914
  30.7 17.6 %collective-permute-start.4 = (f32[232,128]{1,0:T(8,128)}, f32[232,128]{1,0:T(8,128)S(1)}, u32[]{:S(2)}, u32[]{:S(2)}) collective-permute-start(f32[232,128]{1,0:T(8,128)} %get-tuple-element.26), channel_id=1, source_target_pairs={{0,5},{1,6},{2,7},{3,0},{4,1},{5,2},{6,3},{7,4},{8,13},{9,14},{10,... | collective-permute-start | bytes 356360 | tf_op jit(solution)/shard_map/ppermute | solution.py:914
  32.7 15.6 %collective-permute-start.5 = (f32[232,128]{1,0:T(8,128)}, f32[232,128]{1,0:T(8,128)S(1)}, u32[]{:S(2)}, u32[]{:S(2)}) collective-permute-start(f32[232,128]{1,0:T(8,128)} %get-tuple-element.27), channel_id=1, source_target_pairs={{0,6},{1,7},{2,0},{3,1},{4,2},{5,3},{6,4},{7,5},{8,14},{9,15},{10,... | collective-permute-start | bytes 356360 | tf_op jit(solution)/shard_map/ppermute | solution.py:914
  34.0 14.3 %collective-permute-start.6 = (f32[232,128]{1,0:T(8,128)}, f32[232,128]{1,0:T(8,128)S(1)}, u32[]{:S(2)}, u32[]{:S(2)}) collective-permute-start(f32[232,128]{1,0:T(8,128)} %get-tuple-element.28), channel_id=1, source_target_pairs={{0,7},{1,0},{2,1},{3,2},{4,3},{5,4},{6,5},{7,6},{8,15},{9,8},{10,9... | collective-permute-start | bytes 356360 | tf_op jit(solution)/shard_map/ppermute | solution.py:914
  48.4 0.9 %copy-start.2 = (f32[232,128]{1,0:T(8,128)S(1)}, f32[232,128]{1,0:T(8,128)}, u32[]{:S(2)}) copy-start(f32[232,128]{1,0:T(8,128)} %get-tuple-element.21.refs_0_) | copy-start | bytes 356356
